TPU v7x, 32 devices: a whole 2x2x4 slice. The times are simulated.
32 devices in a mesh: member: 2 (over y), lon: 8 (over z, x), lat: 2 (over core).
Axes of the slice: x: 2, y: 2, z: 4, core: 2. Of those that a mesh axis runs over, the one named last changes fastest.
Arguments:
- state_tokens: bfloat16 [8, 24, 96, 768], P('member', 'lat', 'lon'), parts along dimension 0, may hold values from -32 to 32
- land_mask: int32 [24, 96], P('lat', 'lon'), may hold values 0 or 1
- pad_mask: int32 [24], replicated, may hold values from 0 to 1, as said below
- land_embed: float32 [2, 768], replicated, may hold values from -3 to 3
- w_qkv: bfloat16 [768, 1152], replicated, may hold values from -0.21875 to 0.21875
- w_proj: bfloat16 [384, 768], replicated, may hold values from -0.3125 to 0.3125
- proj_bias: float32 [768], replicated, may hold values from -4 to 4
- norm_gain: float32 [768], replicated, may hold values from 0.5 to 1.5
- norm_shift: float32 [768], replicated, may hold values from -1.5 to 1.5
- bias_table: bfloat16 [4, 2, 12, 3312], P('lat'), may hold values from -3.5 to 320
- index_table: int32 [144, 144], replicated, may hold values from 0 to 3311
Outputs:
- result: bfloat16 [8, 24, 96, 768], P('member', 'lat', 'lon'), parts along dimension 0
There are 2 independent parts, one for each index of `member`. A program takes and returns all parts, laid end to end along the dimension named above; an argument that names none is the same for every part. Nothing has to cross between parts.
Inputs may be any that keep to these rules, and one draw needn't show every extreme that they name: pad_mask is 1 on every row except at most the first 2 and the last 2 of the 24 rows, which are 0 where padded; one of the two ends has exactly 2 padding rows.
All inputs are finite; a program needn't handle non-finite values. No bound on the sum of `land_mask` on one device may be relied on, other than what follows from the above.
Results may differ from a plain program's by a relative error of at most 0.0085.
Values may be sent and summed in bfloat16 or wider, within the bound.
No kernel may reach another device: no remote copies, remote signals or barrier semaphores. Data moves between devices by JAX's collectives and lax.ppermute only.
A program may use at most 64 MiB of HBM per device.

v0:
```python
import jax
import jax.numpy as jnp
from jax import lax
from jax.sharding import PartitionSpec as P

HEADS = 12
HEAD_DIM = 32
WIN_Z = 2
WIN_LAT = 6
WIN_LON = 12
WIN_TOK = 144


norm_epsilon = 1e-05


def from_behind(shard, axis, by):
    size = lax.axis_size(axis)
    return lax.ppermute(shard, axis, [(i, (i + by) % size) for i in range(size)])


def as_sent(shard):

    def short(part):
        return part.astype(jnp.bfloat16) if part.dtype == jnp.float32 else part

    return jax.tree.map(short, shard)


def region_of(position, length, window):
    half_window = window // 2
    return jnp.where(
        position < length - window, 0, jnp.where(position < length - half_window, 1, 2)
    ).astype(jnp.int32)


def window_rules(levels, lat_start, lat_rows, lat_total, pad_mask):
    tokens = jnp.arange(WIN_TOK, dtype=jnp.int32)
    level_offset = tokens // (WIN_LAT * WIN_LON)
    row_offset = tokens // WIN_LON % WIN_LAT
    level_index = (
        jnp.arange(levels // WIN_Z, dtype=jnp.int32)[:, None] * WIN_Z + level_offset[None, :]
    )
    row_index = (
        lat_start
        + jnp.arange(lat_rows // WIN_LAT, dtype=jnp.int32)[:, None] * WIN_LAT
        + row_offset[None, :]
    )
    region = (
        region_of(level_index, levels, WIN_Z)[:, None, :] * 3
        + region_of(row_index, lat_total, WIN_LAT)[None, :, :]
    )
    source_row = (row_index + WIN_LAT // 2) % lat_total
    lookup = (
        source_row[:, :, None] == jnp.arange(lat_total, dtype=jnp.int32)[None, None, :]
    ).astype(jnp.int32)
    usable = jnp.sum(lookup * pad_mask[None, None, :], axis=-1) == 1
    return (region[:, :, :, None] == region[:, :, None, :]) & usable[None, :, None, :]


def earth_bias(bias_table, index_table):
    lat_windows, z_windows, heads, positions = bias_table.shape
    table_rows = bias_table.reshape(lat_windows * z_windows * heads, positions).T
    picked = jnp.take(table_rows, index_table.reshape(-1), axis=0)
    picked = picked.reshape(WIN_TOK, WIN_TOK, lat_windows, z_windows, heads).astype(jnp.float32)
    return jnp.transpose(picked, (3, 2, 4, 0, 1))


def to_windows(layout):
    levels, lat_rows, lon_columns, channels = layout.shape
    shaped = layout.reshape(
        levels // WIN_Z,
        WIN_Z,
        lat_rows // WIN_LAT,
        WIN_LAT,
        lon_columns // WIN_LON,
        WIN_LON,
        channels,
    )
    shaped = shaped.transpose(0, 2, 4, 1, 3, 5, 6)
    return shaped.reshape(
        levels // WIN_Z, lat_rows // WIN_LAT, lon_columns // WIN_LON, WIN_TOK, channels
    )


def from_windows(window_tiles):
    z_windows, lat_windows, lon_windows, tokens, channels = window_tiles.shape
    shaped = window_tiles.reshape(
        z_windows, lat_windows, lon_windows, WIN_Z, WIN_LAT, WIN_LON, channels
    )
    shaped = shaped.transpose(0, 3, 1, 4, 2, 5, 6)
    return shaped.reshape(z_windows * WIN_Z, lat_windows * WIN_LAT, lon_windows * WIN_LON, channels)


def attend(windows, bias_full, allowed):
    pieces = windows.reshape(windows.shape[:-1] + (3, HEADS, HEAD_DIM))
    queries = pieces[..., 0, :, :]
    key_rows = pieces[..., 1, :, :]
    value_rows = pieces[..., 2, :, :]
    scores = jnp.einsum(
        "abcthd,abcuhd->abchtu", queries, key_rows, preferred_element_type=jnp.float32
    )
    scores = scores / jnp.sqrt(jnp.float32(HEAD_DIM)) + bias_full[:, :, None]
    scores = jnp.where(allowed[:, :, None, None], scores, -jnp.inf)
    largest = jnp.max(scores, axis=-1, keepdims=True)
    powers = jnp.exp(scores - largest)
    weights = (powers / jnp.sum(powers, axis=-1, keepdims=True)).astype(jnp.bfloat16)
    attended = jnp.einsum(
        "abchtu,abcuhd->abcthd", weights, value_rows, preferred_element_type=jnp.float32
    ).astype(jnp.bfloat16)
    return attended.reshape(attended.shape[:4] + (HEADS * HEAD_DIM,))


def finish(attended, w_proj, proj_bias, norm_gain, norm_shift):
    projected = jnp.dot(attended, w_proj, preferred_element_type=jnp.float32) + proj_bias
    average = jnp.mean(projected, axis=-1, keepdims=True)
    centered = projected - average
    spread = jnp.mean(centered * centered, axis=-1, keepdims=True)
    return centered * lax.rsqrt(spread + norm_epsilon) * norm_gain + norm_shift


def on_device(
    state_tokens,
    land_mask,
    pad_mask,
    land_embed,
    w_qkv,
    w_proj,
    proj_bias,
    norm_gain,
    norm_shift,
    bias_table,
    index_table,
):
    levels, lat_rows, lon_columns, features = state_tokens.shape
    lat_total = lat_rows * lax.axis_size("lat")
    lat_start = lax.axis_index("lat") * lat_rows
    level_half = WIN_Z // 2
    lat_half = WIN_LAT // 2
    lon_half = WIN_LON // 2
    embedded = jnp.where(land_mask[:, :, None] == 1, land_embed[1], land_embed[0])
    hidden = (state_tokens.astype(jnp.float32) + embedded[None]).astype(jnp.bfloat16)
    own_rows = jnp.dot(hidden, w_qkv, preferred_element_type=jnp.float32).astype(jnp.bfloat16)
    rolled = jnp.roll(own_rows, -level_half, axis=0)
    incoming = from_behind(rolled[:, :, :lon_half], "lon", -1)
    rolled = jnp.concatenate([rolled[:, :, lon_half:], incoming], axis=2)
    incoming = from_behind(rolled[:, :lat_half], "lat", -1)
    projections = jnp.concatenate([rolled[:, lat_half:], incoming], axis=1)
    bias_full = earth_bias(bias_table, index_table)
    allowed = window_rules(levels, lat_start, lat_rows, lat_total, pad_mask)
    attended = from_windows(attend(to_windows(projections), bias_full, allowed))
    normed = finish(attended, w_proj, proj_bias, norm_gain, norm_shift)
    incoming = from_behind(normed[:, -lat_half:].astype(jnp.bfloat16), "lat", 1).astype(jnp.float32)
    normed = jnp.concatenate([incoming, normed[:, :-lat_half]], axis=1)
    incoming = from_behind(as_sent(normed[:, :, -lon_half:]), "lon", 1)
    normed = jnp.concatenate([incoming, normed[:, :, :-lon_half]], axis=2)
    normed = jnp.roll(normed, level_half, axis=0)
    return (hidden.astype(jnp.float32) + normed).astype(jnp.bfloat16)


def solution(mesh):
    in_specs = (
        P("member", "lat", "lon", None),
        P("lat", "lon"),
        P(),
        P(),
        P(),
        P(),
        P(),
        P(),
        P(),
        P("lat", None, None, None),
        P(),
    )
    out_specs = P("member", "lat", "lon", None)
    return jax.shard_map(
        on_device, mesh=mesh, in_specs=in_specs, out_specs=out_specs, check_vma=False
    )
```

profile of v0, /device:TPU:0, one launch (start us, length us, event | category | flops | bytes accessed | tf_op | source)
XLA Modules:
  0.0 160.7 jit_solution(6752801541054168498)
XLA Ops:
  0.0 0.9 slice_reduce_fusion.1
  0.9 0.7 broadcast_compare_fusion
  1.6 0.1 broadcast_select_fusion.2
  1.7 0.8 copy-done.2
  2.5 2.9 %convolution_convert_fusion = bf16[4,12,12,1152]{3,2,1,0:T(8,128)(2,1)S(1)} fusion(bf16[768,1152]{1,0:T(8,128)(2,1)S(1)} %copy-done, bf16[4,12,12,768]{3,0,2,1:T(4,128)(2,1)} %param.11, f32[12,12,768]{2,1,0:T(8,128)S(1)} %broadcast_select_fusion.2), kind=kOutput, calls=%fused_computation.12 | convolution fusion | flops 1021206528 | bytes 4423680 | tf_op jit(solution)/shard_map/dot_general | solution.py:143
  5.4 0.1 slice.76
  5.6 0.4 fusion.18
  6.0 0.3 copy.66
  6.3 6.2 %collective-permute-start = (bf16[4,12,6,1152]{3,0,2,1:T(4,128)(2,1)S(1)}, bf16[4,12,6,1152]{3,0,2,1:T(4,128)(2,1)S(1)}, u32[]{:S(2)}, u32[]{:S(2)}) collective-permute-start(bf16[4,12,6,1152]{3,0,2,1:T(4,128)(2,1)S(1)} %copy.66), channel_id=1, source_target_pairs={{0,14},{2,0},{4,2},{6,4},{8,6},{10,8},{12,10},{14,12},{1,15},{3,1}... | collective-permute-start | bytes 1990664 | tf_op jit(solution)/shard_map/ppermute | solution.py:19
  12.8 0.2 reshape.255
  13.1 0.3 fusion.33
  13.4 13.4 %collective-permute-done = bf16[4,12,6,1152]{3,0,2,1:T(4,128)(2,1)S(1)} collective-permute-done((bf16[4,12,6,1152]{3,0,2,1:T(4,128)(2,1)S(1)}, bf16[4,12,6,1152]{3,0,2,1:T(4,128)(2,1)S(1)}, u32[]{:S(2)}, u32[]{:S(2)}) %collective-permute-start) | collective-permute-done | bytes 663584 | tf_op jit(solution)/shard_map/ppermute | solution.py:19
  26.7 0.1 copy.67
  26.8 0.9 pad_maximum_fusion.6
  27.8 0.8 compare_and_fusion
  28.6 1.0 copy.73
  29.7 0.1 reshape.254
  29.8 0.4 copy.74
  30.2 42.0 %gather_fusion = bf16[20736,48]{1,0:T(8,128)(2,1)} fusion(bf16[3312,48]{1,0:T(8,128)(2,1)S(1)} %bitcast.64, s32[21504]{0:T(1024)S(1)} %pad_clamp_fusion), kind=kCustom, calls=%fused_computation | custom fusion | bytes 4064256 | tf_op jit(solution)/shard_map/jit(_take)/gather | solution.py:64
  72.2 6.0 %copy.75 = bf16[20736,48]{0,1:T(8,128)(2,1)} copy(bf16[20736,48]{1,0:T(8,128)(2,1)} %gather_fusion) | data formatting | bytes 3981312 | tf_op jit(solution)/shard_map/jit(_take)/gather | solution.py:64
  78.2 8.2 %gather.7 = bf16[144,144,2,2,12]{1,0,4,3,2:T(8,128)(2,1)} reshape(bf16[20736,48]{0,1:T(8,128)(2,1)} %copy.75) | data formatting | bytes 3981312 | tf_op jit(solution)/shard_map/jit(_take)/gather | solution.py:64
  86.4 6.2 %copy.76 = bf16[144,144,2,2,12]{0,1,4,2,3:T(8,128)(2,1)} copy(bf16[144,144,2,2,12]{1,0,4,3,2:T(8,128)(2,1)} %gather.7) | data formatting | bytes 3981312 | tf_op jit(solution)/shard_map/jit(_take)/gather | solution.py:64
  92.6 0.1 copy.72
  92.8 0.4 fusion.14
  93.2 0.3 pad_maximum_fusion.4
  93.5 1.0 copy.98
  94.6 6.7 %reshape_reshape.6 = bf16[2,2,1,144,3,12,32]{6,5,4,1,3,0,2:T(8,128)(2,1)} reshape(bf16[2,2,1,2,6,12,1152]{6,1,5,4,3,0,2:T(2,128)(2,1)S(1)} %bitcast.66) | data formatting | bytes 2654208 | tf_op jit(solution)/shard_map/reshape;reshape | solution.py:96
  101.3 6.7 %fusion.45 = (bf16[2,2,1,144,1,12,32]{6,5,4,1,3,0,2:T(8,128)(2,1)}, bf16[2,2,1,144,1,12,32]{6,5,4,1,3,0,2:T(8,128)(2,1)}, bf16[2,2,1,144,1,12,32]{6,5,4,1,3,0,2:T(8,128)(2,1)}) fusion(bf16[2,2,1,144,3,12,32]{6,5,4,1,3,0,2:T(8,128)(2,1)} %reshape_reshape.6), kind=kLoop, calls=%fused_computation.89 | loop fusion | bytes 2654208 | tf_op jit(solution)/shard_map/slice | solution.py:99
  107.9 3.3 %copy.90 = bf16[2,2,1,144,1,12,32]{3,6,5,1,0,4,2:T(8,128)(2,1)S(1)} copy(bf16[2,2,1,144,1,12,32]{6,5,4,1,3,0,2:T(8,128)(2,1)} %get-tuple-element.8) | data formatting | bytes 884736
  111.3 3.4 %copy.91 = bf16[2,2,1,144,1,12,32]{3,6,5,1,0,4,2:T(8,128)(2,1)S(1)} copy(bf16[2,2,1,144,1,12,32]{6,5,4,1,3,0,2:T(8,128)(2,1)} %get-tuple-element.9) | data formatting | bytes 884736
  114.7 3.6 %copy.89 = bf16[2,2,1,144,1,12,32]{3,6,5,1,0,4,2:T(8,128)(2,1)S(1)} copy(bf16[2,2,1,144,1,12,32]{6,5,4,1,3,0,2:T(8,128)(2,1)} %get-tuple-element.7) | data formatting | bytes 884736
  118.3 8.1 %fusion.46 = (f32[2,2,12,144]{3,2,1,0:T(8,128)S(1)}, f32[2,2,12,144,144]{3,4,2,1,0:T(8,128)}) fusion(pred[2,2,144,144]{2,3,1,0:T(8,128)(4,1)S(1)} %copy-done.7, bf16[144,144,2,2,12]{0,1,4,2,3:T(8,128)(2,1)} %copy.76, pred[144,144]{0,1:T(8,128)(4,1)S(1)} %copy.72, bf16[2,2,1,144,1,12,32]{3,6,5,1,0,4,2:T(8,128)(2,1)S(1)} %copy.91, ...), kind=kOutput, calls=%fused_computation.90 | convolution fusion | flops 70668432 | bytes 6988032 | tf_op jit(solution)/shard_map/sub | solution.py:106
  126.4 3.6 %fusion.15 = bf16[2,2,1,144,12,32]{3,5,4,1,0,2:T(8,128)(2,1)S(1)} fusion(f32[2,2,12,144,144]{3,4,2,1,0:T(8,128)} %get-tuple-element.15, f32[2,2,12,144]{3,2,1,0:T(8,128)S(1)} %get-tuple-element.14, bf16[2,2,1,144,1,12,32]{3,6,5,1,0,4,2:T(8,128)(2,1)S(1)} %copy.89), kind=kOutput, calls=%fused_computation.36 | convolution fusion | flops 65912832 | bytes 4893696 | tf_op jit(solution)/shard_map/abchtu,abcuhd->abcthd/dot_general | solution.py:108
  130.0 4.2 %copy.78 = bf16[2,2,1,144,12,32]{5,4,1,3,0,2:T(8,128)(2,1)} copy(bf16[2,2,1,144,12,32]{3,5,4,1,0,2:T(8,128)(2,1)S(1)} %fusion.15) | data formatting | bytes 884736 | tf_op jit(solution)/shard_map/convert_element_type | solution.py:110
  134.2 3.7 %reshape_reshape.7 = bf16[2,2,1,2,6,12,384]{6,1,5,4,3,0,2:T(2,128)(2,1)S(1)} reshape(bf16[2,2,1,144,12,32]{5,4,1,3,0,2:T(8,128)(2,1)} %copy.78) | data formatting | bytes 884736 | tf_op jit(solution)/shard_map/reshape;reshape | solution.py:88
  138.0 0.8 add_reduce_fusion
  138.9 0.5 multiply_reduce_fusion
  139.4 0.5 multiply_add_fusion
  140.0 0.6 collective-permute-start.2
  140.5 0.1 slice.86
  140.7 1.1 collective-permute-done.2
  141.8 0.2 fusion.17
  142.0 0.3 copy.81
  142.4 0.4 collective-permute-start.3
  142.7 15.5 %collective-permute-done.3 = bf16[4,12,6,768]{3,0,2,1:T(4,128)(2,1)S(1)} collective-permute-done((bf16[4,12,6,768]{3,0,2,1:T(4,128)(2,1)S(1)}, bf16[4,12,6,768]{3,0,2,1:T(4,128)(2,1)S(1)}, u32[]{:S(2)}, u32[]{:S(2)}) %collective-permute-start.3) | collective-permute-done | bytes 442400 | tf_op jit(solution)/shard_map/ppermute | solution.py:19
  158.3 0.1 copy_convert_fusion
  158.4 0.6 fusion.10
  159.1 1.6 copy.83
  (41 shorter events, 0.6 us)
Async XLA Ops:
  0.0 2.5 %copy-start = (bf16[768,1152]{1,0:T(8,128)(2,1)S(1)}, bf16[768,1152]{1,0:T(8,128)(2,1)}, u32[]{:S(2)}) copy-start(bf16[768,1152]{1,0:T(8,128)(2,1)} %param.15) | copy-start | bytes 5308420
  1.7 0.8 copy-start.2
  5.6 7.1 %copy-start.11 = (s32[24]{0:T(128)S(1)}, s32[24]{0:T(128)}, u32[]{:S(2)}) copy-start(s32[24]{0:T(128)} %param.13) | copy-start | bytes 292
  5.6 7.2 %copy-start.5 = (s32[144,144]{1,0:T(8,128)S(1)}, s32[144,144]{1,0:T(8,128)}, u32[]{:S(2)}) copy-start(s32[144,144]{1,0:T(8,128)} %param.21) | copy-start | bytes 248836
  6.3 20.4 %collective-permute-start = (bf16[4,12,6,1152]{3,0,2,1:T(4,128)(2,1)S(1)}, bf16[4,12,6,1152]{3,0,2,1:T(4,128)(2,1)S(1)}, u32[]{:S(2)}, u32[]{:S(2)}) collective-permute-start(bf16[4,12,6,1152]{3,0,2,1:T(4,128)(2,1)S(1)} %copy.66), channel_id=1, source_target_pairs={{0,14},{2,0},{4,2},{6,4},{8,6},{10,8},{12,10},{14,12},{1,15},{3,1}... | collective-permute-start | bytes 1990664 | tf_op jit(solution)/shard_map/ppermute | solution.py:19
  27.8 65.4 %collective-permute-start.1 = (bf16[4,3,12,1152]{3,2,1,0:T(8,128)(2,1)}, bf16[4,3,12,1152]{3,2,1,0:T(8,128)(2,1)S(1)}, u32[]{:S(2)}, u32[]{:S(2)}) collective-permute-start(bf16[4,3,12,1152]{3,2,1,0:T(8,128)(2,1)} %pad_maximum_fusion.6), channel_id=1, source_target_pairs={{0,1},{1,0},{2,3},{3,2},{4,5},{5,4},{6,7},{7,6},{8,9},{9,8},{10,11... | collective-permute-start | bytes 995336 | tf_op jit(solution)/shard_map/ppermute | solution.py:19
  114.7 3.6 %copy-start.7 = (pred[2,2,144,144]{2,3,1,0:T(8,128)(4,1)S(1)}, pred[2,2,144,144]{2,3,1,0:T(8,128)(4,1)}, u32[]{:S(2)}) copy-start(pred[2,2,144,144]{2,3,1,0:T(8,128)(4,1)} %compare_and_fusion) | copy-start | bytes 248836
  134.2 3.8 %copy-start.6 = (bf16[384,768]{1,0:T(8,128)(2,1)S(1)}, bf16[384,768]{1,0:T(8,128)(2,1)}, u32[]{:S(2)}) copy-start(bf16[384,768]{1,0:T(8,128)(2,1)} %param.16) | copy-start | bytes 1769476
  134.2 3.8 %copy-start.8 = (f32[768]{0:T(1024)S(1)}, f32[768]{0:T(1024)}, u32[]{:S(2)}) copy-start(f32[768]{0:T(1024)} %param.17) | copy-start | bytes 9220
  138.0 1.4 copy-start.9
  138.0 1.4 copy-start.10
  140.0 1.8 %collective-permute-start.2 = (bf16[4,3,12,768]{3,2,1,0:T(8,128)(2,1)S(1)}, bf16[4,3,12,768]{3,2,1,0:T(8,128)(2,1)S(1)}, u32[]{:S(2)}, u32[]{:S(2)}) collective-permute-start(bf16[4,3,12,768]{3,2,1,0:T(8,128)(2,1)S(1)} %slice.112), channel_id=1, source_target_pairs={{0,1},{1,0},{2,3},{3,2},{4,5},{5,4},{6,7},{7,6},{8,9},{9,8},{10,11... | collective-permute-start | bytes 663560 | tf_op jit(solution)/shard_map/ppermute | solution.py:19
  141.8 16.6 %copy-start.3 = (f32[12,12,768]{2,1,0:T(8,128)S(1)}, f32[12,12,768]{2,1,0:T(8,128)}, u32[]{:S(2)}) copy-start(f32[12,12,768]{2,1,0:T(8,128)} %copy-done.2) | copy-start | bytes 1327108
  141.8 16.6 %copy-start.4 = (bf16[4,12,12,768]{3,0,2,1:T(4,128)(2,1)S(1)}, bf16[4,12,12,768]{3,0,2,1:T(4,128)(2,1)}, u32[]{:S(2)}) copy-start(bf16[4,12,12,768]{3,0,2,1:T(4,128)(2,1)} %param.11) | copy-start | bytes 2654212
  142.4 15.9 %collective-permute-start.3 = (bf16[4,12,6,768]{3,0,2,1:T(4,128)(2,1)S(1)}, bf16[4,12,6,768]{3,0,2,1:T(4,128)(2,1)S(1)}, u32[]{:S(2)}, u32[]{:S(2)}) collective-permute-start(bf16[4,12,6,768]{3,0,2,1:T(4,128)(2,1)S(1)} %copy.81), channel_id=1, source_target_pairs={{0,2},{2,4},{4,6},{6,8},{8,10},{10,12},{12,14},{14,0},{1,3},{3,5},... | collective-permute-start | bytes 1327112 | tf_op jit(solution)/shard_map/ppermute | solution.py:19
  158.4 2.3 %copy-start.1 = (bf16[768,1152]{1,0:T(8,128)(2,1)S(1)}, bf16[768,1152]{1,0:T(8,128)(2,1)}, u32[]{:S(2)}) copy-start(bf16[768,1152]{1,0:T(8,128)(2,1)} %param.15) | copy-start | bytes 5308420
where the time goes:
time: 161 us
  local copies, waits for them, and re-layouts  101 us (63%)
  waiting for transfers between devices  30 us (19%)
  matrix products  15.5 us (10%)
  starting transfers between devices  7.21 us (4%)
  other arithmetic  6.19 us (4%)
    gather x4, local copies, waits for them, and re-layouts, earth_bias(): picked = jnp.take(table_rows, index_table.reshape(-1), axis=0)  62.4 us
    ppermute x4, waiting for transfers between devices, from_behind(): lax.ppermute(shard, axis, [(i, (i + by) % size) for i in range(size)])  30 us
    unnamed x28, local copies, waits for them, and re-layouts  12.2 us
    sub x1, matrix products, attend(): powers = jnp.exp(scores - largest)  8.11 us
    ppermute x4, starting transfers between devices, from_behind(): lax.ppermute(shard, axis, [(i, (i + by) % size) for i in range(size)])  7.21 us
    another operation x1, local copies, waits for them, and re-layouts, attend(): pieces = windows.reshape(windows.shape[:-1] + (3, HEADS, HEAD_DIM))  6.7 us
    slice x1, local copies, waits for them, and re-layouts, attend(): value_rows = pieces[..., 2, :, :]  6.66 us
    convert_element_type x1, local copies, waits for them, and re-layouts, attend(): attended = jnp.einsum('abchtu,abcuhd->abcthd', weights, value_rows, prefe...  4.18 us
  transfers between devices with their start and end apart: 4, of which 3 were waited for; matrix products, arithmetic and copies ran while one was open for 41% of the time, Pallas kernels for 0%

commit v1 on v0

v1 whole, which is shorter than its diff:
```python
import functools

import jax
import jax.numpy as jnp
from jax import lax
from jax.experimental import pallas as pl
from jax.experimental.pallas import tpu as pltpu
from jax.sharding import PartitionSpec as P

HEADS = 12
HEAD_DIM = 32
WIN_Z = 2
WIN_LAT = 6
WIN_LON = 12
WIN_TOK = 144
HALF_TOK = 72
LANES = 128
REST = WIN_TOK - LANES
LOW = 256

norm_epsilon = 1e-05


def from_behind(shard, axis, by):
    size = lax.axis_size(axis)
    return lax.ppermute(shard, axis, [(i, (i + by) % size) for i in range(size)])


def region_of(position, length, window):
    half_window = window // 2
    return jnp.where(
        position < length - window, 0, jnp.where(position < length - half_window, 1, 2)
    ).astype(jnp.int32)


def half_major(table, axis):
    shape = table.shape
    half = WIN_LON // 2
    split = shape[:axis] + (WIN_Z * WIN_LAT, 2, half) + shape[axis + 1:]
    return jnp.swapaxes(table.reshape(split), axis, axis + 1).reshape(shape)


def window_rules(levels, lat_start, lat_rows, lat_total, pad_mask):
    tokens = jnp.arange(HALF_TOK, dtype=jnp.int32)
    half = WIN_LON // 2
    level_offset = jnp.tile(tokens // (WIN_LAT * half), 2)
    row_offset = jnp.tile(tokens // half % WIN_LAT, 2)
    level_index = (
        jnp.arange(levels // WIN_Z, dtype=jnp.int32)[:, None] * WIN_Z + level_offset[None, :]
    )
    row_index = (
        lat_start
        + jnp.arange(lat_rows // WIN_LAT, dtype=jnp.int32)[:, None] * WIN_LAT
        + row_offset[None, :]
    )
    region = (
        region_of(level_index, levels, WIN_Z)[:, None, :] * 3
        + region_of(row_index, lat_total, WIN_LAT)[None, :, :]
    )
    source_row = (row_index + WIN_LAT // 2) % lat_total
    lookup = (
        source_row[:, :, None] == jnp.arange(lat_total, dtype=jnp.int32)[None, None, :]
    ).astype(jnp.int32)
    usable = jnp.sum(lookup * pad_mask[None, None, :], axis=-1) == 1
    key_code = jnp.where(usable[None], region, -1)
    return key_code[:, :, :, None], region[:, :, None, :]


def bias_kernel(table_ref, low_ref, high_ref, main_ref, rest_ref, *, tables, chunks, main_tiles, rest_tiles):
    position = lax.broadcasted_iota(jnp.int32, (LOW, LOW), 0)

    def pick(i):
        one_hot = jnp.where(position == low_ref[i], 1.0, 0.0).astype(jnp.bfloat16)
        found = jnp.dot(table_ref[...], one_hot, preferred_element_type=jnp.float32)
        high = high_ref[i]
        chosen = found[:tables]
        for c in range(1, chunks):
            chosen = jnp.where(high == c, found[c * tables:(c + 1) * tables], chosen)
        return chosen

    def main_step(i, carry):
        chosen = pick(i)
        main_ref[pl.ds(2 * i, tables, stride=WIN_TOK), :] = chosen[:, :LANES]
        main_ref[pl.ds(2 * i + 1, tables, stride=WIN_TOK), :] = chosen[:, LANES:]
        return carry

    def rest_step(i, carry):
        chosen = pick(main_tiles + i)
        per_half = LANES // REST
        for j in range(2 * per_half):
            part = chosen[:, :LANES] if j < per_half else chosen[:, LANES:]
            shift = (j % per_half) * REST
            if shift:
                part = pltpu.roll(part, LANES - shift, 1)
            rest_ref[pl.ds(2 * per_half * i + j, tables, stride=WIN_TOK), :] = part
        return carry

    lax.fori_loop(0, main_tiles, main_step, 0)
    lax.fori_loop(0, rest_tiles, rest_step, 0)


def earth_bias(bias_table, index_table):
    lat_windows, z_windows, heads, positions = bias_table.shape
    tables = lat_windows * z_windows * heads
    chunks = -(-positions // LOW)
    rows = bias_table.reshape(tables, positions)
    rows = jnp.pad(rows, ((0, 0), (0, chunks * LOW - positions)))
    rows = jnp.swapaxes(rows.reshape(tables, chunks, LOW), 0, 1).reshape(chunks * tables, LOW)
    index = half_major(half_major(index_table.T, 0), 1)
    main = index[:, :LANES].reshape(-1, 1, LOW)
    rest = index[:, LANES:].reshape(-1, 1, LOW)
    index = jnp.concatenate([main, rest], axis=0)
    out = jax.ShapeDtypeStruct((tables * WIN_TOK, LANES), jnp.float32)
    main_bias, rest_bias = pl.pallas_call(
        functools.partial(
            bias_kernel, tables=tables, chunks=chunks,
            main_tiles=main.shape[0], rest_tiles=rest.shape[0],
        ),
        out_shape=(out, out),
        compiler_params=pltpu.CompilerParams(vmem_limit_bytes=40 << 20),
        cost_estimate=pl.CostEstimate(
            flops=2 * chunks * tables * LOW * WIN_TOK * WIN_TOK,
            transcendentals=0, bytes_accessed=8 << 20,
        ),
        name="bias_lookup",
    )(rows, index % LOW, index // LOW)
    shape = (lat_windows, z_windows, heads, WIN_TOK, LANES)
    return main_bias.reshape(shape), rest_bias.reshape(shape)


def attend_kernel(
    own_ref, halo_ref, w_qkv_ref, main_ref, rest_ref, key_ref, query_ref, w_proj_ref,
    proj_bias_ref, gain_ref, shift_ref, out_own_ref, out_halo_ref, qkv_own, qkv_halo, attended_ref,
):
    windows = own_ref.shape[0]
    features = own_ref.shape[2]
    width = HEADS * HEAD_DIM
    qkv_own[...] = jnp.dot(
        own_ref[...].reshape(windows * HALF_TOK, features), w_qkv_ref[...],
        preferred_element_type=jnp.float32,
    )
    qkv_halo[...] = jnp.dot(
        halo_ref[...].reshape(windows * HALF_TOK, features), w_qkv_ref[...],
        preferred_element_type=jnp.float32,
    )
    scale = 1.0 / (HEAD_DIM ** 0.5)
    per_group = LANES // HEAD_DIM
    for w in range(windows):
        rows = slice(w * HALF_TOK, (w + 1) * HALF_TOK)
        qkv = jnp.concatenate([qkv_own[rows], qkv_halo[rows]], axis=0)
        queries = qkv[:, :width].T.astype(jnp.bfloat16)
        key_rows = qkv[:, width:2 * width].astype(jnp.bfloat16)
        value_rows = qkv[:, 2 * width:].T.astype(jnp.bfloat16)
        allowed = key_ref[w] == query_ref[w]
        pieces = []
        for h in range(HEADS):
            group, spot = h // per_group, h % per_group
            query = queries[h * HEAD_DIM:(h + 1) * HEAD_DIM]
            blocks = [jnp.zeros((HEAD_DIM, WIN_TOK), jnp.bfloat16)] * per_group
            blocks[spot] = query
            scores = jnp.dot(
                key_rows[:, group * LANES:(group + 1) * LANES], jnp.concatenate(blocks, axis=0),
                preferred_element_type=jnp.float32,
            )
            bias = jnp.concatenate([main_ref[w, h], rest_ref[w, h][:, :REST]], axis=1)
            scores = jnp.where(allowed, scores * scale + bias, -1e30)
            powers = jnp.exp(scores - jnp.max(scores, axis=0, keepdims=True))
            weights = powers * (1.0 / jnp.sum(powers, axis=0, keepdims=True))
            pieces.append(jnp.dot(
                value_rows[h * HEAD_DIM:(h + 1) * HEAD_DIM], weights.astype(jnp.bfloat16),
                preferred_element_type=jnp.float32,
            ))
        attended_ref[w * WIN_TOK:(w + 1) * WIN_TOK] = (
            jnp.concatenate(pieces, axis=0).T.astype(jnp.bfloat16)
        )
    projected = jnp.dot(
        attended_ref[...], w_proj_ref[...], preferred_element_type=jnp.float32
    ) + proj_bias_ref[...]
    average = jnp.mean(projected, axis=-1, keepdims=True)
    centered = projected - average
    spread = jnp.mean(centered * centered, axis=-1, keepdims=True)
    normed = centered * lax.rsqrt(spread + norm_epsilon) * gain_ref[...] + shift_ref[...]
    for w in range(windows):
        start = w * WIN_TOK
        out_own_ref[w] = normed[start:start + HALF_TOK].astype(jnp.bfloat16)
        out_halo_ref[w] = normed[start + HALF_TOK:start + WIN_TOK].astype(jnp.bfloat16)


def attend(own, halo, z, w_qkv, bias, codes, w_proj, proj_bias, norm_gain, norm_shift):
    windows, _, features = own.shape
    main_bias, rest_bias = bias

    def whole(a):
        return pl.BlockSpec(a.shape, lambda i: (0,) * a.ndim)

    bias_spec = pl.BlockSpec((windows, None, HEADS, WIN_TOK, LANES), lambda i: (0, z, 0, 0, 0))
    rows = [v.reshape(1, features) for v in (proj_bias, norm_gain, norm_shift)]
    args = (own, halo, w_qkv, main_bias, rest_bias, codes[0][z], codes[1][z], w_proj, *rows)
    specs = [whole(a) for a in args]
    specs[3] = specs[4] = bias_spec
    out = jax.ShapeDtypeStruct(own.shape, jnp.bfloat16)
    width = HEADS * HEAD_DIM
    return pl.pallas_call(
        attend_kernel,
        out_shape=(out, out),
        grid=(1,),
        in_specs=specs,
        out_specs=[whole(out), whole(out)],
        scratch_shapes=[
            pltpu.VMEM((windows * HALF_TOK, 3 * width), jnp.float32),
            pltpu.VMEM((windows * HALF_TOK, 3 * width), jnp.float32),
            pltpu.VMEM((windows * WIN_TOK, width), jnp.bfloat16),
        ],
        compiler_params=pltpu.CompilerParams(vmem_limit_bytes=48 << 20),
        cost_estimate=pl.CostEstimate(
            flops=6 * 10 ** 9, transcendentals=10 ** 6, bytes_accessed=8 << 20
        ),
        name="window_attention",
    )(*args)


def to_windows(layout):
    levels, lat_rows, columns, channels = layout.shape
    shaped = layout.reshape(
        levels // WIN_Z, WIN_Z, lat_rows // WIN_LAT, WIN_LAT, columns, channels
    )
    shaped = shaped.transpose(0, 2, 1, 3, 4, 5)
    return shaped.reshape(levels // WIN_Z, lat_rows // WIN_LAT, HALF_TOK, channels)


def from_windows(tiles):
    z_windows, lat_windows, _, channels = tiles.shape
    shaped = tiles.reshape(z_windows, lat_windows, WIN_Z, WIN_LAT, WIN_LON // 2, channels)
    shaped = shaped.transpose(0, 2, 1, 3, 4, 5)
    return shaped.reshape(z_windows * WIN_Z, lat_windows * WIN_LAT, WIN_LON // 2, channels)


def on_device(
    state_tokens,
    land_mask,
    pad_mask,
    land_embed,
    w_qkv,
    w_proj,
    proj_bias,
    norm_gain,
    norm_shift,
    bias_table,
    index_table,
):
    levels, lat_rows, lon_columns, features = state_tokens.shape
    lat_total = lat_rows * lax.axis_size("lat")
    lat_start = lax.axis_index("lat") * lat_rows
    level_half = WIN_Z // 2
    lat_half = WIN_LAT // 2
    lon_half = WIN_LON // 2

    def embed(tokens, mask):
        embedded = jnp.where(mask[:, :, None] == 1, land_embed[1], land_embed[0])
        return (tokens.astype(jnp.float32) + embedded[None]).astype(jnp.bfloat16)

    def shift_rows(part):
        rolled = jnp.roll(part, -level_half, axis=0)
        incoming = from_behind(rolled[:, :lat_half], "lat", -1)
        return to_windows(jnp.concatenate([rolled[:, lat_half:], incoming], axis=1))

    first = embed(state_tokens[:, :, :lon_half], land_mask[:, :lon_half])
    halo = from_behind(first, "lon", -1)
    last = embed(state_tokens[:, :, lon_half:], land_mask[:, lon_half:])
    own_windows = shift_rows(last)
    bias = earth_bias(bias_table, index_table)
    codes = window_rules(levels, lat_start, lat_rows, lat_total, pad_mask)
    halo_windows = shift_rows(halo)
    kept, returned = [], []
    for z in range(levels // WIN_Z):
        own_out, halo_out = attend(
            own_windows[z], halo_windows[z], z, w_qkv, bias, codes,
            w_proj, proj_bias, norm_gain, norm_shift,
        )
        kept.append(own_out)
        returned.append(from_behind(halo_out, "lon", 1))

    def unshift_rows(tiles):
        layout = from_windows(tiles)
        incoming = from_behind(layout[:, -lat_half:], "lat", 1)
        layout = jnp.concatenate([incoming, layout[:, :-lat_half]], axis=1)
        return jnp.roll(layout, level_half, axis=0).astype(jnp.float32)

    result_last = (last.astype(jnp.float32) + unshift_rows(jnp.stack(kept))).astype(jnp.bfloat16)
    result_first = (first.astype(jnp.float32) + unshift_rows(jnp.stack(returned))).astype(jnp.bfloat16)
    return jnp.concatenate([result_first, result_last], axis=2)


def solution(mesh):
    in_specs = (
        P("member", "lat", "lon", None),
        P("lat", "lon"),
        P(),
        P(),
        P(),
        P(),
        P(),
        P(),
        P(),
        P("lat", None, None, None),
        P(),
    )
    out_specs = P("member", "lat", "lon", None)
    return jax.shard_map(
        on_device, mesh=mesh, in_specs=in_specs, out_specs=out_specs, check_vma=False
    )
```

time: 161 us -> 95.3 us (0.59)
  local copies, waits for them, and re-layouts: 101 us -> 19.5 us
  Pallas kernels: 0 us -> 40.2 us
  matrix products: 15.5 us -> 0 us
  waiting for transfers between devices: 30 us -> 15.8 us
  other arithmetic: 6.19 us -> 12.2 us
    gather x4 -> x0, local copies, waits for them, and re-layouts: 62.4 us -> none  [earth_bias(): picked = jnp.take(table_rows, index_table.reshape(-1), axis=0)]
    pallas_call x0 -> x3, Pallas kernels: none -> 40.2 us  [the longest x1 23 us: earth_bias(): pl.pallas_call(functools.partial(bias_kernel, tables=tables, chunks=chunk...]
    ppermute x4 -> x7, waiting for transfers between devices: 30 us -> 15.8 us  [from_behind(): lax.ppermute(shard, axis, [(i, (i + by) % size) for i in range(size)])]
    sub x1 -> x0, matrix products: 8.11 us -> none  [attend(): powers = jnp.exp(scores - largest)]
    another operation x2 -> x3, local copies, waits for them, and re-layouts: 10.4 us -> 2.35 us  [the longest x1 2.35 us: half_major(): return jnp.swapaxes(table.reshape(split), axis, axis + 1).reshape(shape)]
    unnamed x28 -> x25, local copies, waits for them, and re-layouts: 12.2 us -> 4.24 us
    dot_general x3 -> x0, matrix products: 7.38 us -> none  [the longest x1 3.61 us: attend(): jnp.einsum('abchtu,abcuhd->abcthd', weights, value_rows, preferred_elemen...]
    convert_element_type x2 -> x0, local copies, waits for them, and re-layouts: 5.78 us -> none  [the longest x1 4.18 us: attend(): attended = jnp.einsum('abchtu,abcuhd->abcthd', weights, value_rows, prefe...]
  transfers between devices with their start and end apart: 4 -> 7, of which waited for: 3 -> 5; matrix products, arithmetic and copies ran while one was open for 41% -> 9% of each run, Pallas kernels for 0% -> 24%
where the time goes in v1:
time: 95.3 us; the launch traced here: 95 us
  Pallas kernels  40.2 us (42%)
  local copies, waits for them, and re-layouts  19.5 us (20%)
  waiting for transfers between devices  15.8 us (17%)
  other arithmetic  12.2 us (13%)
  starting transfers between devices  6.67 us (7%)
    pallas_call x1, Pallas kernels, earth_bias(): pl.pallas_call(functools.partial(bias_kernel, tables=tables, chunks=chunk...  23 us
    pallas_call x2, Pallas kernels, attend(): pl.pallas_call(attend_kernel, out_shape=(out, out), grid=(1,), in_specs=s...  17.2 us
    ppermute x7, waiting for transfers between devices, from_behind(): lax.ppermute(shard, axis, [(i, (i + by) % size) for i in range(size)])  15.8 us
    ppermute x7, starting transfers between devices, from_behind(): lax.ppermute(shard, axis, [(i, (i + by) % size) for i in range(size)])  6.67 us
    unnamed x25, local copies, waits for them, and re-layouts  4.24 us
    reshape x4, local copies, waits for them, and re-layouts, to_windows(): layout.reshape(levels // WIN_Z, WIN_Z, lat_rows // WIN_LAT, WIN_LAT, colu...  3.84 us
    slice x4, local copies, waits for them, and re-layouts, shift_rows(): rolled = jnp.roll(part, -level_half, axis=0)  2.97 us
    convert_element_type x1, other arithmetic, embed(): return (tokens.astype(jnp.float32) + embedded[None]).astype(jnp.bfloat16)  2.41 us
  transfers between devices with their start and end apart: 7, of which 5 were waited for; matrix products, arithmetic and copies ran while one was open for 9% of the time, Pallas kernels for 24%

profile of v1, /device:TPU:0, one launch (start us, length us, event | category | flops | bytes accessed | tf_op | source)
XLA Modules:
  0.0 95.0 jit_solution(496143084057333938)
XLA Ops:
  0.0 0.8 slice_reduce_fusion.1
  0.8 0.8 slice_compare_fusion.1
  1.8 2.4 %add_convert_fusion.3 = (bf16[4,12,6,768]{3,0,2,1:T(4,128)(2,1)}, bf16[4,12,6,768]{3,0,2,1:T(4,128)(2,1)S(1)}) fusion(f32[12,6,768]{2,1,0:T(8,128)S(1)} %get-tuple-element.27, bf16[4,12,12,768]{3,0,2,1:T(4,128)(2,1)} %param.11, f32[12,6,768]{2,1,0:T(8,128)S(1)} %get-tuple-element.28), kind=kLoop, calls=%fused_computation.4 | loop fusion | flops 1327104 | bytes 2211840 | tf_op jit(solution)/shard_map/convert_element_type | solution.py:260
  4.3 0.6 copy-done.4
  4.9 0.2 slice.142
  5.3 0.6 collective-permute-start
  5.9 5.6 %collective-permute-start.1 = (bf16[4,12,6,768]{3,0,2,1:T(4,128)(2,1)}, bf16[4,12,6,768]{3,0,2,1:T(4,128)(2,1)}, u32[]{:S(2)}, u32[]{:S(2)}) collective-permute-start(bf16[4,12,6,768]{3,0,2,1:T(4,128)(2,1)} %get-tuple-element.21), channel_id=1, source_target_pairs={{0,14},{2,0},{4,2},{6,4},{8,6},{10,8},{12,10},{14,12},{1,15},{3,1}... | collective-permute-start | bytes 1327112 | tf_op jit(solution)/shard_map/ppermute | solution.py:26
  11.6 2.3 %reshape_reshape.3 = s32[144,12,2,6]{3,2,1,0:T(2,128)S(1)} reshape(s32[2,12,6,144]{3,2,1,0:T(8,128)S(1)} %copy.65) | data formatting | bytes 165888 | tf_op jit(solution)/shard_map/reshape;reshape | solution.py:40
  14.0 1.2 %copy.66 = s32[144,2,12,6]{0,3,2,1:T(8,128)S(1)} copy(s32[144,2,12,6]{3,1,2,0:T(2,128)S(1)} %bitcast.49) | data formatting | bytes 165888 | tf_op jit(solution)/shard_map/transpose | solution.py:40
  15.5 0.2 reshape.528
  16.2 0.4 and_select_fusion
  17.5 23.0 %bias_lookup.1 = (f32[6912,128]{1,0:T(8,128)S(1)}, f32[6912,128]{1,0:T(8,128)S(1)}) custom-call(bf16[624,256]{1,0:T(8,128)(2,1)S(1)} %bitcast.44, s32[81,1,256]{2,1,0:T(1,128)S(1)} %and_select_fusion.1.low_ref, s32[81,1,256]{2,1,0:T(1,128)S(1)} %get-tuple-element.19.high_ref), custom_call_target="tpu_custom_call" | custom-call | flops 6624903168 | bytes 8388608 | tf_op jit(solution)/shard_map/bias_lookup/pallas_call | solution.py:114
  40.5 1.8 %copy-done.2 = f32[6912,128]{1,0:T(8,128)} copy-done((f32[6912,128]{1,0:T(8,128)}, f32[6912,128]{1,0:T(8,128)S(1)}, u32[]{:S(2)}) %copy-start.2) | copy-done | bytes 3538968
  42.3 1.8 %copy-done.3 = f32[6912,128]{1,0:T(8,128)} copy-done((f32[6912,128]{1,0:T(8,128)}, f32[6912,128]{1,0:T(8,128)S(1)}, u32[]{:S(2)}) %copy-start.3) | copy-done | bytes 3538968
  44.1 0.3 fusion.3
  44.4 0.3 pad_maximum_fusion.3
  44.7 0.2 reshape.525
  44.9 0.3 copy.85
  45.2 0.3 fusion.10
  45.7 1.3 %slice.148 = bf16[1,12,6,768]{3,0,2,1:T(2,128)(2,1)S(1)} slice(bf16[4,12,6,768]{3,0,2,1:T(4,128)(2,1)} %collective-permute-done.1), slice={[0:1], [0:12], [0:6], [0:768]} | slice | bytes 221184 | tf_op jit(solution)/shard_map/jit(_roll_static)/slice | solution.py:263
  47.0 1.3 %slice.147 = bf16[3,12,6,768]{3,0,2,1:T(4,128)(2,1)S(1)} slice(bf16[4,12,6,768]{3,0,2,1:T(4,128)(2,1)} %collective-permute-done.1), slice={[1:4], [0:12], [0:6], [0:768]} | slice | bytes 663552 | tf_op jit(solution)/shard_map/jit(_roll_static)/slice | solution.py:263
  48.4 0.2 collective-permute-start.2
  48.6 0.3 fusion.2
  48.9 0.8 collective-permute-done.2
  49.8 1.1 %pad_maximum_fusion.4 = bf16[4,12,6,768]{3,0,2,1:T(4,128)(2,1)} fusion(bf16[4,3,6,768]{3,0,2,1:T(4,128)(2,1)S(1)} %collective-permute-done.2, bf16[4,9,6,768]{3,0,2,1:T(4,128)(2,1)S(1)} %fusion.2), kind=kLoop, calls=%fused_computation.14 | loop fusion | flops 221184 | bytes 884736 | tf_op jit(solution)/shard_map/concatenate | solution.py:265
  50.8 2.0 %reshape.526 = bf16[2,2,2,6,6,768]{5,1,0,4,3,2:T(2,128)(2,1)} reshape(bf16[4,12,6,768]{3,0,2,1:T(4,128)(2,1)} %pad_maximum_fusion.4) | data formatting | bytes 884736 | tf_op jit(solution)/shard_map/reshape | solution.py:224
  52.8 1.4 %copy.84 = bf16[2,2,2,6,6,768]{5,2,4,3,1,0:T(2,128)(2,1)S(1)} copy(bf16[2,2,2,6,6,768]{5,1,0,4,3,2:T(2,128)(2,1)} %reshape.526) | data formatting | bytes 884736 | tf_op jit(solution)/shard_map/reshape | solution.py:224
  54.2 0.3 fusion.9
  54.5 8.5 %window_attention.3 = (bf16[2,72,768]{2,1,0:T(8,128)(2,1)S(1)}, bf16[2,72,768]{2,1,0:T(8,128)(2,1)S(1)}) custom-call(bf16[2,72,768]{2,1,0:T(8,128)(2,1)S(1)} %copy.74.own_ref, bf16[2,72,768]{2,1,0:T(8,128)(2,1)S(1)} %copy.75.halo_ref, bf16[768,1152]{1,0:T(8,128)(2,1)S(1)} %copy-done, f32[2,2,12,144,128]{4,3,2,1,0:T(8,128)} %bitcast.45, ...), custom_call_target="tpu_custom_call" | custom-call | flops 6000000000 | bytes 8388608 | tf_op jit(solution)/shard_map/window_attention/pallas_call | solution.py:203
  63.0 0.2 copy.80
  63.2 8.7 %window_attention.2 = (bf16[2,72,768]{2,1,0:T(8,128)(2,1)S(1)}, bf16[2,72,768]{2,1,0:T(8,128)(2,1)S(1)}) custom-call(bf16[2,72,768]{2,1,0:T(8,128)(2,1)S(1)} %copy.70.own_ref, bf16[2,72,768]{2,1,0:T(8,128)(2,1)S(1)} %copy.71.halo_ref, bf16[768,1152]{1,0:T(8,128)(2,1)S(1)} %copy-done, f32[2,2,12,144,128]{4,3,2,1,0:T(8,128)} %bitcast.46, ...), custom_call_target="tpu_custom_call" | custom-call | flops 6000000000 | bytes 8388608 | tf_op jit(solution)/shard_map/window_attention/pallas_call | solution.py:203
  72.0 0.2 copy.79
  72.2 0.6 maximum_bitcast_fusion.1
  72.8 0.3 copy.81
  73.4 0.2 collective-permute-start.6
  73.7 1.0 %collective-permute-done.6 = bf16[4,3,6,768]{3,0,2,1:T(4,128)(2,1)S(1)} collective-permute-done((bf16[4,3,6,768]{3,0,2,1:T(4,128)(2,1)S(1)}, bf16[4,3,6,768]{3,0,2,1:T(4,128)(2,1)S(1)}, u32[]{:S(2)}, u32[]{:S(2)}) %collective-permute-start.6) | collective-permute-done | bytes 110624 | tf_op jit(solution)/shard_map/ppermute | solution.py:26
  74.8 0.4 fusion.4
  75.2 9.4 %collective-permute-done.4 = bf16[2,72,768]{2,1,0:T(8,128)(2,1)S(1)} collective-permute-done((bf16[2,72,768]{2,1,0:T(8,128)(2,1)S(1)}, bf16[2,72,768]{2,1,0:T(8,128)(2,1)S(1)}, u32[]{:S(2)}, u32[]{:S(2)}) %collective-permute-start.4) | collective-permute-done | bytes 221216 | tf_op jit(solution)/shard_map/ppermute | solution.py:26
  84.6 0.2 copy.77
  84.8 3.9 %collective-permute-done.3 = bf16[2,72,768]{2,1,0:T(8,128)(2,1)S(1)} collective-permute-done((bf16[2,72,768]{2,1,0:T(8,128)(2,1)S(1)}, bf16[2,72,768]{2,1,0:T(8,128)(2,1)S(1)}, u32[]{:S(2)}, u32[]{:S(2)}) %collective-permute-start.3) | collective-permute-done | bytes 221216 | tf_op jit(solution)/shard_map/ppermute | solution.py:26
  88.7 0.2 copy.73
  88.9 0.6 maximum_bitcast_fusion
  89.5 0.3 copy.78
  90.2 0.6 add_convert_fusion
  90.9 0.6 collective-permute-done.5
  91.5 0.4 fusion.5
  91.9 1.6 %add_convert_fusion.1 = bf16[4,12,6,768]{3,0,2,1:T(4,128)(2,1)S(1)} fusion(bf16[4,12,6,768]{3,0,2,1:T(4,128)(2,1)} %get-tuple-element.21, bf16[4,9,6,768]{3,0,2,1:T(4,128)(2,1)S(1)} %slice.161, bf16[4,3,6,768]{3,0,2,1:T(4,128)(2,1)S(1)} %collective-permute-done.5, bf16[1,12,6,768]{3,0,2,1:T(2,128)(2,1)S(1)} %fusion.5), kind=kLoop, calls=%fused_computation.2 | loop fusion | flops 1990656 | bytes 1437696 | tf_op jit(solution)/shard_map/convert_element_type | solution.py:290
  93.5 1.5 %pad_maximum_fusion = bf16[4,12,12,768]{3,0,2,1:T(4,128)(2,1)} fusion(bf16[4,12,6,768]{3,0,2,1:T(4,128)(2,1)S(1)} %add_convert_fusion, bf16[4,12,6,768]{3,0,2,1:T(4,128)(2,1)S(1)} %add_convert_fusion.1), kind=kLoop, calls=%fused_computation | loop fusion | flops 442368 | bytes 1769472 | tf_op jit(solution)/shard_map/concatenate | solution.py:291
  (73 shorter events, 3.0 us)
Async XLA Ops:
  0.0 11.4 %copy-start.7 = (s32[144,144]{1,0:T(8,128)S(1)}, s32[144,144]{1,0:T(8,128)}, u32[]{:S(2)}) copy-start(s32[144,144]{1,0:T(8,128)} %param.21) | copy-start | bytes 248836
  4.2 0.8 copy-start.4
  4.9 10.4 %copy-start.6 = (bf16[2,2,12,3312]{3,1,2,0:T(2,128)(2,1)S(1)}, bf16[2,2,12,3312]{3,1,2,0:T(2,128)(2,1)}, u32[]{:S(2)}) copy-start(bf16[2,2,12,3312]{3,1,2,0:T(2,128)(2,1)} %param.20) | copy-start | bytes 953860
  5.3 39.1 %collective-permute-start = (bf16[4,3,6,768]{3,0,2,1:T(4,128)(2,1)S(1)}, bf16[4,3,6,768]{3,0,2,1:T(4,128)(2,1)S(1)}, u32[]{:S(2)}, u32[]{:S(2)}) collective-permute-start(bf16[4,3,6,768]{3,0,2,1:T(4,128)(2,1)S(1)} %pad_maximum_fusion.6), channel_id=1, source_target_pairs={{0,1},{1,0},{2,3},{3,2},{4,5},{5,4},{6,7},{7,6},{8,9},{9,8},{10,11... | collective-permute-start | bytes 331784 | tf_op jit(solution)/shard_map/ppermute | solution.py:26
  5.9 39.8 %collective-permute-start.1 = (bf16[4,12,6,768]{3,0,2,1:T(4,128)(2,1)}, bf16[4,12,6,768]{3,0,2,1:T(4,128)(2,1)}, u32[]{:S(2)}, u32[]{:S(2)}) collective-permute-start(bf16[4,12,6,768]{3,0,2,1:T(4,128)(2,1)} %get-tuple-element.21), channel_id=1, source_target_pairs={{0,14},{2,0},{4,2},{6,4},{8,6},{10,8},{12,10},{14,12},{1,15},{3,1}... | collective-permute-start | bytes 1327112 | tf_op jit(solution)/shard_map/ppermute | solution.py:26
  13.9 3.0 %copy-start.11 = (s32[24]{0:T(128)S(1)}, s32[24]{0:T(128)}, u32[]{:S(2)}) copy-start(s32[24]{0:T(128)} %param.13) | copy-start | bytes 292
  14.0 3.3 %copy-start.8 = (f32[768]{0:T(1024)S(1)}, f32[768]{0:T(1024)}, u32[]{:S(2)}) copy-start(f32[768]{0:T(1024)} %param.17) | copy-start | bytes 9220
  14.0 3.4 %copy-start.9 = (f32[768]{0:T(1024)S(1)}, f32[768]{0:T(1024)}, u32[]{:S(2)}) copy-start(f32[768]{0:T(1024)} %param.18) | copy-start | bytes 9220
  14.0 3.4 %copy-start.10 = (f32[768]{0:T(1024)S(1)}, f32[768]{0:T(1024)}, u32[]{:S(2)}) copy-start(f32[768]{0:T(1024)} %param.19) | copy-start | bytes 9220
  40.5 1.8 %copy-start.2 = (f32[6912,128]{1,0:T(8,128)}, f32[6912,128]{1,0:T(8,128)S(1)}, u32[]{:S(2)}) copy-start(f32[6912,128]{1,0:T(8,128)S(1)} %get-tuple-element.11) | copy-start | bytes 10616836
  42.3 1.8 %copy-start.3 = (f32[6912,128]{1,0:T(8,128)}, f32[6912,128]{1,0:T(8,128)S(1)}, u32[]{:S(2)}) copy-start(f32[6912,128]{1,0:T(8,128)S(1)} %get-tuple-element.12) | copy-start | bytes 10616836
  45.6 8.9 %copy-start = (bf16[768,1152]{1,0:T(8,128)(2,1)S(1)}, bf16[768,1152]{1,0:T(8,128)(2,1)}, u32[]{:S(2)}) copy-start(bf16[768,1152]{1,0:T(8,128)(2,1)} %w_qkv_ref.3) | copy-start | bytes 5308420
  45.6 8.9 %copy-start.1 = (bf16[384,768]{1,0:T(8,128)(2,1)S(1)}, bf16[384,768]{1,0:T(8,128)(2,1)}, u32[]{:S(2)}) copy-start(bf16[384,768]{1,0:T(8,128)(2,1)} %w_proj_ref.3) | copy-start | bytes 1769476
  48.4 1.4 %collective-permute-start.2 = (bf16[4,3,6,768]{3,0,2,1:T(4,128)(2,1)S(1)}, bf16[4,3,6,768]{3,0,2,1:T(4,128)(2,1)S(1)}, u32[]{:S(2)}, u32[]{:S(2)}) collective-permute-start(bf16[4,3,6,768]{3,0,2,1:T(4,128)(2,1)S(1)} %pad_maximum_fusion.5), channel_id=1, source_target_pairs={{0,1},{1,0},{2,3},{3,2},{4,5},{5,4},{6,7},{7,6},{8,9},{9,8},{10,11... | collective-permute-start | bytes 331784 | tf_op jit(solution)/shard_map/ppermute | solution.py:26
  72.8 17.4 %copy-start.5 = (bf16[4,12,6,768]{3,0,2,1:T(4,128)(2,1)S(1)}, bf16[4,12,6,768]{3,0,2,1:T(4,128)(2,1)}, u32[]{:S(2)}) copy-start(bf16[4,12,6,768]{3,0,2,1:T(4,128)(2,1)} %copy-done.4) | copy-start | bytes 1327108
  73.4 1.4 %collective-permute-start.6 = (bf16[4,3,6,768]{3,0,2,1:T(4,128)(2,1)S(1)}, bf16[4,3,6,768]{3,0,2,1:T(4,128)(2,1)S(1)}, u32[]{:S(2)}, u32[]{:S(2)}) collective-permute-start(bf16[4,3,6,768]{3,0,2,1:T(4,128)(2,1)S(1)} %slice.164), channel_id=1, source_target_pairs={{0,1},{1,0},{2,3},{3,2},{4,5},{5,4},{6,7},{7,6},{8,9},{9,8},{10,11... | collective-permute-start | bytes 331784 | tf_op jit(solution)/shard_map/ppermute | solution.py:26
  73.6 11.0 %collective-permute-start.4 = (bf16[2,72,768]{2,1,0:T(8,128)(2,1)S(1)}, bf16[2,72,768]{2,1,0:T(8,128)(2,1)S(1)}, u32[]{:S(2)}, u32[]{:S(2)}) collective-permute-start(bf16[2,72,768]{2,1,0:T(8,128)(2,1)S(1)} %get-tuple-element.14), channel_id=1, source_target_pairs={{0,2},{2,4},{4,6},{6,8},{8,10},{10,12},{12,14},{14,0},{1,3},{3,5},... | collective-permute-start | bytes 663560 | tf_op jit(solution)/shard_map/ppermute | solution.py:26
  73.6 15.1 %collective-permute-start.3 = (bf16[2,72,768]{2,1,0:T(8,128)(2,1)S(1)}, bf16[2,72,768]{2,1,0:T(8,128)(2,1)S(1)}, u32[]{:S(2)}, u32[]{:S(2)}) collective-permute-start(bf16[2,72,768]{2,1,0:T(8,128)(2,1)S(1)} %get-tuple-element.13), channel_id=1, source_target_pairs={{0,2},{2,4},{4,6},{6,8},{8,10},{10,12},{12,14},{14,0},{1,3},{3,5},... | collective-permute-start | bytes 663560 | tf_op jit(solution)/shard_map/ppermute | solution.py:26
  90.1 1.4 %collective-permute-start.5 = (bf16[4,3,6,768]{3,0,2,1:T(4,128)(2,1)S(1)}, bf16[4,3,6,768]{3,0,2,1:T(4,128)(2,1)S(1)}, u32[]{:S(2)}, u32[]{:S(2)}) collective-permute-start(bf16[4,3,6,768]{3,0,2,1:T(4,128)(2,1)S(1)} %slice.160), channel_id=1, source_target_pairs={{0,1},{1,0},{2,3},{3,2},{4,5},{5,4},{6,7},{7,6},{8,9},{9,8},{10,11... | collective-permute-start | bytes 331784 | tf_op jit(solution)/shard_map/ppermute | solution.py:26

commit v2 on v1

--- a/solution.py
+++ b/solution.py
@@ -2,6 +2,7 @@
 
 import jax
 import jax.numpy as jnp
+import numpy as np
 from jax import lax
 from jax.experimental import pallas as pl
 from jax.experimental.pallas import tpu as pltpu
@@ -33,18 +34,47 @@
     ).astype(jnp.int32)
 
 
-def half_major(table, axis):
-    shape = table.shape
-    half = WIN_LON // 2
-    split = shape[:axis] + (WIN_Z * WIN_LAT, 2, half) + shape[axis + 1:]
-    return jnp.swapaxes(table.reshape(split), axis, axis + 1).reshape(shape)
+BLOCK = 36
+SLAB = 16
+
+
+def block_major(table):
+    parts = (WIN_Z, 2, WIN_LAT // 2, 2, WIN_LON // 2)
+    split = table.reshape(parts + parts)
+    order = (3, 1, 0, 2, 4)
+    return split.transpose(order + tuple(5 + o for o in order)).reshape(table.shape)
+
+
+def offsets(groups):
+    kept = -(-(groups - 1) * BLOCK // SLAB) * SLAB
+    last = -(-BLOCK // SLAB) * SLAB
+    starts = (0, kept, kept + last, 2 * kept + last)
+    return starts, 2 * (kept + last)
+
+
+def packing(lat_rows):
+    third = WIN_LAT // 2
+    groups = lat_rows // third
+    starts, total = offsets(groups)
+    chosen = np.zeros((total, WIN_Z * lat_rows * SLAB), np.float32)
+    for half in range(2):
+        for group in range(groups):
+            first_row = 0 if group == groups - 1 else third * (group + 1)
+            base = starts[2 * half + 1] if group == groups - 1 else starts[2 * half] + group * BLOCK
+            for level in range(WIN_Z):
+                for row in range(third):
+                    for column in range(WIN_LON // 2):
+                        packed = base + (level * third + row) * (WIN_LON // 2) + column
+                        source = (level * lat_rows + first_row + row) * SLAB
+                        chosen[packed, source + half * (WIN_LON // 2) + column] = 1
+    return chosen
 
 
 def window_rules(levels, lat_start, lat_rows, lat_total, pad_mask):
-    tokens = jnp.arange(HALF_TOK, dtype=jnp.int32)
-    half = WIN_LON // 2
-    level_offset = jnp.tile(tokens // (WIN_LAT * half), 2)
-    row_offset = jnp.tile(tokens // half % WIN_LAT, 2)
+    tokens = jnp.arange(WIN_TOK, dtype=jnp.int32)
+    third = WIN_LAT // 2
+    level_offset = tokens // (BLOCK // WIN_Z) % WIN_Z
+    row_offset = tokens // BLOCK % 2 * third + tokens // (WIN_LON // 2) % third
     level_index = (
         jnp.arange(levels // WIN_Z, dtype=jnp.int32)[:, None] * WIN_Z + level_offset[None, :]
     )
@@ -95,8 +125,8 @@
             rest_ref[pl.ds(2 * per_half * i + j, tables, stride=WIN_TOK), :] = part
         return carry
 
-    lax.fori_loop(0, main_tiles, main_step, 0)
-    lax.fori_loop(0, rest_tiles, rest_step, 0)
+    lax.fori_loop(0, main_tiles, main_step, 0, unroll=8)
+    lax.fori_loop(0, rest_tiles, rest_step, 0, unroll=3)
 
 
 def earth_bias(bias_table, index_table):
@@ -106,7 +136,7 @@
     rows = bias_table.reshape(tables, positions)
     rows = jnp.pad(rows, ((0, 0), (0, chunks * LOW - positions)))
     rows = jnp.swapaxes(rows.reshape(tables, chunks, LOW), 0, 1).reshape(chunks * tables, LOW)
-    index = half_major(half_major(index_table.T, 0), 1)
+    index = block_major(index_table.T)
     main = index[:, :LANES].reshape(-1, 1, LOW)
     rest = index[:, LANES:].reshape(-1, 1, LOW)
     index = jnp.concatenate([main, rest], axis=0)
@@ -129,25 +159,27 @@
 
 
 def attend_kernel(
-    own_ref, halo_ref, w_qkv_ref, main_ref, rest_ref, key_ref, query_ref, w_proj_ref,
-    proj_bias_ref, gain_ref, shift_ref, out_own_ref, out_halo_ref, qkv_own, qkv_halo, attended_ref,
+    own_ref, own_last_ref, halo_ref, halo_last_ref, w_qkv_ref, main_ref, rest_ref, key_ref, query_ref, w_proj_ref,
+    proj_bias_ref, gain_ref, shift_ref, out_own_ref, out_halo_ref, out_last_ref, qkv_ref, attended_ref,
 ):
-    windows = own_ref.shape[0]
-    features = own_ref.shape[2]
+    windows = main_ref.shape[0]
     width = HEADS * HEAD_DIM
-    qkv_own[...] = jnp.dot(
-        own_ref[...].reshape(windows * HALF_TOK, features), w_qkv_ref[...],
-        preferred_element_type=jnp.float32,
-    )
-    qkv_halo[...] = jnp.dot(
-        halo_ref[...].reshape(windows * HALF_TOK, features), w_qkv_ref[...],
-        preferred_element_type=jnp.float32,
+    pieces = []
+    for w in range(windows):
+        for part, last in ((own_ref, own_last_ref), (halo_ref, halo_last_ref)):
+            if w < windows - 1:
+                pieces.append(part[w * HALF_TOK:(w + 1) * HALF_TOK])
+            else:
+                pieces.append(part[w * HALF_TOK:w * HALF_TOK + BLOCK])
+                pieces.append(last[...])
+    tokens = jnp.concatenate([p.astype(jnp.float32) for p in pieces], axis=0)
+    qkv_ref[...] = jnp.dot(
+        tokens.astype(jnp.bfloat16), w_qkv_ref[...], preferred_element_type=jnp.float32
     )
     scale = 1.0 / (HEAD_DIM ** 0.5)
     per_group = LANES // HEAD_DIM
     for w in range(windows):
-        rows = slice(w * HALF_TOK, (w + 1) * HALF_TOK)
-        qkv = jnp.concatenate([qkv_own[rows], qkv_halo[rows]], axis=0)
+        qkv = qkv_ref[w * WIN_TOK:(w + 1) * WIN_TOK]
         queries = qkv[:, :width].T.astype(jnp.bfloat16)
         key_rows = qkv[:, width:2 * width].astype(jnp.bfloat16)
         value_rows = qkv[:, 2 * width:].T.astype(jnp.bfloat16)
@@ -181,34 +213,42 @@
     spread = jnp.mean(centered * centered, axis=-1, keepdims=True)
     normed = centered * lax.rsqrt(spread + norm_epsilon) * gain_ref[...] + shift_ref[...]
     for w in range(windows):
-        start = w * WIN_TOK
-        out_own_ref[w] = normed[start:start + HALF_TOK].astype(jnp.bfloat16)
-        out_halo_ref[w] = normed[start + HALF_TOK:start + WIN_TOK].astype(jnp.bfloat16)
-
-
-def attend(own, halo, z, w_qkv, bias, codes, w_proj, proj_bias, norm_gain, norm_shift):
-    windows, _, features = own.shape
+        for half, out_ref in ((0, out_own_ref), (1, out_halo_ref)):
+            start = w * WIN_TOK + half * HALF_TOK
+            size = HALF_TOK if w < windows - 1 else BLOCK
+            out_ref[w * HALF_TOK:w * HALF_TOK + size] = normed[start:start + size].astype(jnp.bfloat16)
+            if w == windows - 1:
+                out_last_ref[half] = normed[start + BLOCK:start + HALF_TOK].astype(jnp.bfloat16)
+
+
+def whole(a):
+    return pl.BlockSpec(a.shape, lambda i: (0,) * a.ndim)
+
+
+def attend(own, own_last, halo, halo_last, z, w_qkv, bias, codes, w_proj, proj_bias, norm_gain, norm_shift):
+    features = own.shape[-1]
     main_bias, rest_bias = bias
-
-    def whole(a):
-        return pl.BlockSpec(a.shape, lambda i: (0,) * a.ndim)
-
+    windows = main_bias.shape[0]
     bias_spec = pl.BlockSpec((windows, None, HEADS, WIN_TOK, LANES), lambda i: (0, z, 0, 0, 0))
+    part_spec = pl.BlockSpec((None,) + own.shape[1:], lambda i: (z, 0, 0))
+    halo_spec = pl.BlockSpec((None,) + halo.shape[1:], lambda i: (z, 0, 0))
+    own_last_spec = pl.BlockSpec((None, None) + own_last.shape[2:], lambda i: (z, 1, 0, 0))
+    halo_last_spec = pl.BlockSpec((None,) + halo_last.shape[1:], lambda i: (z, 0, 0))
     rows = [v.reshape(1, features) for v in (proj_bias, norm_gain, norm_shift)]
-    args = (own, halo, w_qkv, main_bias, rest_bias, codes[0][z], codes[1][z], w_proj, *rows)
-    specs = [whole(a) for a in args]
-    specs[3] = specs[4] = bias_spec
-    out = jax.ShapeDtypeStruct(own.shape, jnp.bfloat16)
+    args = (own, own_last, halo, halo_last, w_qkv, main_bias, rest_bias, codes[0][z], codes[1][z], w_proj, *rows)
+    specs = [part_spec, own_last_spec, halo_spec, halo_last_spec, whole(w_qkv), bias_spec, bias_spec]
+    specs += [whole(a) for a in args[len(specs):]]
+    out = jax.ShapeDtypeStruct(own.shape[1:], jnp.bfloat16)
+    out_last = jax.ShapeDtypeStruct((2, BLOCK, features), jnp.bfloat16)
     width = HEADS * HEAD_DIM
     return pl.pallas_call(
         attend_kernel,
-        out_shape=(out, out),
+        out_shape=(out, out, out_last),
         grid=(1,),
         in_specs=specs,
-        out_specs=[whole(out), whole(out)],
+        out_specs=[whole(out), whole(out), whole(out_last)],
         scratch_shapes=[
-            pltpu.VMEM((windows * HALF_TOK, 3 * width), jnp.float32),
-            pltpu.VMEM((windows * HALF_TOK, 3 * width), jnp.float32),
+            pltpu.VMEM((windows * WIN_TOK, 3 * width), jnp.float32),
             pltpu.VMEM((windows * WIN_TOK, width), jnp.bfloat16),
         ],
         compiler_params=pltpu.CompilerParams(vmem_limit_bytes=48 << 20),
@@ -219,20 +259,77 @@
     )(*args)
 
 
-def to_windows(layout):
-    levels, lat_rows, columns, channels = layout.shape
-    shaped = layout.reshape(
-        levels // WIN_Z, WIN_Z, lat_rows // WIN_LAT, WIN_LAT, columns, channels
-    )
-    shaped = shaped.transpose(0, 2, 1, 3, 4, 5)
-    return shaped.reshape(levels // WIN_Z, lat_rows // WIN_LAT, HALF_TOK, channels)
-
-
-def from_windows(tiles):
-    z_windows, lat_windows, _, channels = tiles.shape
-    shaped = tiles.reshape(z_windows, lat_windows, WIN_Z, WIN_LAT, WIN_LON // 2, channels)
-    shaped = shaped.transpose(0, 2, 1, 3, 4, 5)
-    return shaped.reshape(z_windows * WIN_Z, lat_windows * WIN_LAT, WIN_LON // 2, channels)
+def shifted_levels(z, levels):
+    return [(WIN_Z * z + d + WIN_Z // 2) % levels for d in range(WIN_Z)]
+
+
+def pack_kernel(state_ref, mask_ref, embed_ref, chosen_ref, first_ref, own_ref, last_ref, hidden_ref):
+    levels, lat_rows, columns, features = state_ref.shape
+    groups = lat_rows // (WIN_LAT // 2)
+    starts, _ = offsets(groups)
+    kept = first_ref.shape[1]
+    hidden_ref[...] = jnp.zeros_like(hidden_ref)
+    for i in range(lat_rows):
+        embedded = jnp.where(mask_ref[:, i:i + 1] == 1, embed_ref[1:2], embed_ref[0:1])
+        for z in range(levels):
+            hidden = (state_ref[z, i].astype(jnp.float32) + embedded).astype(jnp.bfloat16)
+            hidden_ref[z, i, :columns] = hidden
+    for z in range(levels // WIN_Z):
+        slabs = [
+            hidden_ref[l].reshape(lat_rows * SLAB, features) for l in shifted_levels(z, levels)
+        ]
+        packed = jnp.dot(
+            chosen_ref[...], jnp.concatenate(slabs, axis=0), preferred_element_type=jnp.float32
+        ).astype(jnp.bfloat16)
+        first_ref[z] = packed[:kept]
+        last_ref[z, 0] = packed[starts[1]:starts[1] + BLOCK]
+        own_ref[z] = packed[starts[2]:starts[2] + kept]
+        last_ref[z, 1] = packed[starts[3]:starts[3] + BLOCK]
+
+
+def pack(state_tokens, land_mask, land_embed):
+    levels, lat_rows, _, features = state_tokens.shape
+    z_windows = levels // WIN_Z
+    kept = (lat_rows // (WIN_LAT // 2) - 1) * BLOCK
+    part = jax.ShapeDtypeStruct((z_windows, kept, features), jnp.bfloat16)
+    return pl.pallas_call(
+        pack_kernel,
+        out_shape=(
+            part, part,
+            jax.ShapeDtypeStruct((z_windows, 2, BLOCK, features), jnp.bfloat16),
+            jax.ShapeDtypeStruct((levels, lat_rows, SLAB, features), jnp.bfloat16),
+        ),
+        compiler_params=pltpu.CompilerParams(vmem_limit_bytes=32 << 20),
+        name="embed_and_pack",
+    )(state_tokens, land_mask.T, land_embed, jnp.asarray(packing(lat_rows), jnp.bfloat16))
+
+
+def unpack_kernel(hidden_ref, chosen_ref, *refs):
+    result_ref, packed_ref = refs[-2:]
+    levels, lat_rows, columns, features = result_ref.shape
+    starts, _ = offsets(lat_rows // (WIN_LAT // 2))
+    packed_ref[...] = jnp.zeros_like(packed_ref)
+    for z in range(levels // WIN_Z):
+        for start, ref in zip(starts, refs[4 * z:4 * z + 4]):
+            packed_ref[z, start:start + ref.shape[0]] = ref[...]
+        placed = jnp.dot(chosen_ref[...], packed_ref[z], preferred_element_type=jnp.float32)
+        for d, l in enumerate(shifted_levels(z, levels)):
+            rows = lat_rows * SLAB
+            hidden = hidden_ref[l].reshape(rows, features).astype(jnp.float32)
+            total_rows = (hidden + placed[d * rows:(d + 1) * rows]).astype(jnp.bfloat16)
+            result_ref[l] = total_rows.reshape(lat_rows, SLAB, features)[:, :columns]
+
+
+def unpack(hidden, parts, shape):
+    levels, lat_rows, _, features = shape
+    _, total = offsets(lat_rows // (WIN_LAT // 2))
+    return pl.pallas_call(
+        unpack_kernel,
+        out_shape=jax.ShapeDtypeStruct(shape, jnp.bfloat16),
+        scratch_shapes=[pltpu.VMEM((levels // WIN_Z, total, features), jnp.bfloat16)],
+        compiler_params=pltpu.CompilerParams(vmem_limit_bytes=32 << 20),
+        name="unpack_and_add",
+    )(hidden, jnp.asarray(packing(lat_rows).T, jnp.bfloat16), *parts)
 
 
 def on_device(
@@ -248,47 +345,31 @@
     bias_table,
     index_table,
 ):
-    levels, lat_rows, lon_columns, features = state_tokens.shape
+    levels, lat_rows, _, _ = state_tokens.shape
     lat_total = lat_rows * lax.axis_size("lat")
     lat_start = lax.axis_index("lat") * lat_rows
-    level_half = WIN_Z // 2
-    lat_half = WIN_LAT // 2
-    lon_half = WIN_LON // 2
-
-    def embed(tokens, mask):
-        embedded = jnp.where(mask[:, :, None] == 1, land_embed[1], land_embed[0])
-        return (tokens.astype(jnp.float32) + embedded[None]).astype(jnp.bfloat16)
-
-    def shift_rows(part):
-        rolled = jnp.roll(part, -level_half, axis=0)
-        incoming = from_behind(rolled[:, :lat_half], "lat", -1)
-        return to_windows(jnp.concatenate([rolled[:, lat_half:], incoming], axis=1))
-
-    first = embed(state_tokens[:, :, :lon_half], land_mask[:, :lon_half])
+    z_windows = levels // WIN_Z
+    first, own, last, hidden = pack(state_tokens, land_mask, land_embed)
     halo = from_behind(first, "lon", -1)
-    last = embed(state_tokens[:, :, lon_half:], land_mask[:, lon_half:])
-    own_windows = shift_rows(last)
+    last = from_behind(last, "lat", -1)
+    halo_last = from_behind(last[:, 0], "lon", -1)
     bias = earth_bias(bias_table, index_table)
     codes = window_rules(levels, lat_start, lat_rows, lat_total, pad_mask)
-    halo_windows = shift_rows(halo)
-    kept, returned = [], []
-    for z in range(levels // WIN_Z):
-        own_out, halo_out = attend(
-            own_windows[z], halo_windows[z], z, w_qkv, bias, codes,
+    kept, returned, lasts = [], [], []
+    for z in range(z_windows):
+        own_out, halo_out, last_out = attend(
+            own, last, halo, halo_last, z, w_qkv, bias, codes,
             w_proj, proj_bias, norm_gain, norm_shift,
         )
         kept.append(own_out)
         returned.append(from_behind(halo_out, "lon", 1))
-
-    def unshift_rows(tiles):
-        layout = from_windows(tiles)
-        incoming = from_behind(layout[:, -lat_half:], "lat", 1)
-        layout = jnp.concatenate([incoming, layout[:, :-lat_half]], axis=1)
-        return jnp.roll(layout, level_half, axis=0).astype(jnp.float32)
-
-    result_last = (last.astype(jnp.float32) + unshift_rows(jnp.stack(kept))).astype(jnp.bfloat16)
-    result_first = (first.astype(jnp.float32) + unshift_rows(jnp.stack(returned))).astype(jnp.bfloat16)
-    return jnp.concatenate([result_first, result_last], axis=2)
+        lasts.append(last_out)
+    turned = from_behind(jnp.stack(lasts), "lat", 1)
+    corner = from_behind(turned[:, 1], "lon", 1)
+    parts = []
+    for z in range(z_windows):
+        parts += [returned[z], corner[z], kept[z], turned[z, 0]]
+    return unpack(hidden, parts, state_tokens.shape)
 
 
 def solution(mesh):

time: 95.3 us -> 85.4 us (0.90)
  other arithmetic: 12.2 us -> 0.75 us
  Pallas kernels: 40.2 us -> 30.1 us
  local copies, waits for them, and re-layouts: 19.5 us -> 27.7 us
  waiting for transfers between devices: 15.8 us -> 19.2 us
    pallas_call x1, Pallas kernels: 23 us -> 10.3 us  [earth_bias(): pl.pallas_call(functools.partial(bias_kernel, tables=tables, chunks=chunk...]
    reshape x8 -> x3, local copies, waits for them, and re-layouts: 4.23 us -> 13.5 us  [the longest x2 10.9 us: block_major(): split = table.reshape(parts + parts)]
    unnamed x25 -> x31, local copies, waits for them, and re-layouts: 4.24 us -> 8.93 us
    slice x11 -> x0, local copies, waits for them, and re-layouts: 4.68 us -> none  [the longest x4 2.97 us: shift_rows(): rolled = jnp.roll(part, -level_half, axis=0)]
    concatenate x9 -> x0, other arithmetic: 4.59 us -> none  [the longest x1 1.49 us: on_device(): return jnp.concatenate([result_first, result_last], axis=2)]
    convert_element_type x3 -> x0, other arithmetic: 4.58 us -> none  [the longest x1 2.41 us: embed(): return (tokens.astype(jnp.float32) + embedded[None]).astype(jnp.bfloat16)]
    ppermute x7, waiting for transfers between devices: 15.8 us -> 19.2 us  [from_behind(): lax.ppermute(shard, axis, [(i, (i + by) % size) for i in range(size)])]
    pallas_call x2 -> x4, Pallas kernels: 17.2 us -> 19.8 us  [the longest x2 17.4 us: attend(): pl.pallas_call(attend_kernel, out_shape=(out, out, out_last), grid=(1,),...]
  transfers between devices with their start and end apart: 7 -> 7, of which waited for: 5 -> 3; matrix products, arithmetic and copies ran while one was open for 9% -> 21% of each run, Pallas kernels for 24% -> 12%
where the time goes in v2:
time: 85.4 us; the launch traced here: 85.1 us
  Pallas kernels  30.1 us (35%)
  local copies, waits for them, and re-layouts  27.7 us (32%)
  waiting for transfers between devices  19.2 us (22%)
  starting transfers between devices  7.02 us (8%)
    ppermute x7, waiting for transfers between devices, from_behind(): lax.ppermute(shard, axis, [(i, (i + by) % size) for i in range(size)])  19.2 us
    pallas_call x2, Pallas kernels, attend(): pl.pallas_call(attend_kernel, out_shape=(out, out, out_last), grid=(1,),...  17.4 us
    reshape x2, local copies, waits for them, and re-layouts, block_major(): split = table.reshape(parts + parts)  10.9 us
    pallas_call x1, Pallas kernels, earth_bias(): pl.pallas_call(functools.partial(bias_kernel, tables=tables, chunks=chunk...  10.3 us
    unnamed x31, local copies, waits for them, and re-layouts  8.93 us
    ppermute x7, starting transfers between devices, from_behind(): lax.ppermute(shard, axis, [(i, (i + by) % size) for i in range(size)])  7.02 us
    reshape x1, local copies, waits for them, and re-layouts, block_major(): split.transpose(order + tuple((5 + o for o in order))).reshape(table.shape)  2.6 us
  transfers between devices with their start and end apart: 7, of which 3 were waited for; matrix products, arithmetic and copies ran while one was open for 21% of the time, Pallas kernels for 12%

profile of v2, /device:TPU:0, one launch (start us, length us, event | category | flops | bytes accessed | tf_op | source)
XLA Modules:
  0.0 85.1 jit_solution(18136878962539991673)
XLA Ops:
  0.0 0.8 copy.35
  0.8 1.3 %copy.36.state_ref = bf16[4,12,12,768]{3,2,1,0:T(8,128)(2,1)S(1)} copy(bf16[4,12,12,768]{3,0,2,1:T(4,128)(2,1)} %param.13) | data formatting | bytes 1769472 | tf_op args[0]
  2.2 1.6 %embed_and_pack.1 = (bf16[2,108,768]{2,1,0:T(8,128)(2,1)}, bf16[2,108,768]{2,1,0:T(8,128)(2,1)S(1)}, bf16[2,2,36,768]{3,2,1,0:T(8,128)(2,1)S(1)}, bf16[4,12,16,768]{3,2,1,0:T(8,128)(2,1)S(1)}) custom-call(bf16[4,12,12,768]{3,2,1,0:T(8,128)(2,1)S(1)} %copy.36.state_ref, s32[12,12]{1,0:T(8,128)S(1)} %bitcast.35, f32[2,768]{1,0:T(2,128)S(1)} %copy-done.2, ...), custom_call_target="tpu_custom_call" | custom-call | tf_op jit(solution)/shard_map/embed_and_pack/pallas_call | solution.py:295
  3.8 0.8 copy.37
  4.6 0.1 copy-done.5
  4.7 0.5 collective-permute-start
  5.2 5.5 %collective-permute-start.1 = (bf16[2,108,768]{2,1,0:T(8,128)(2,1)}, bf16[2,108,768]{2,1,0:T(8,128)(2,1)}, u32[]{:S(2)}, u32[]{:S(2)}) collective-permute-start(bf16[2,108,768]{2,1,0:T(8,128)(2,1)} %get-tuple-element.20), channel_id=1, source_target_pairs={{0,14},{2,0},{4,2},{6,4},{8,6},{10,8},{12,10},{14,12},{1,15},{3,1}... | collective-permute-start | bytes 995336 | tf_op jit(solution)/shard_map/ppermute | solution.py:27
  10.7 3.6 %reshape.514 = s32[2,2,3,2,6,2,2,3,2,6]{4,3,2,1,0,9,8,7,6,5:T(2,128)} reshape(s32[144,144]{0,1:T(8,128)S(1)} %bitcast.43) | data formatting | bytes 165888 | tf_op jit(solution)/shard_map/reshape | solution.py:43
  14.3 7.4 %copy.40 = s32[2,2,3,2,6,2,2,3,2,6]{9,7,5,6,8,4,2,0,1,3:T(4,128)S(1)} copy(s32[2,2,3,2,6,2,2,3,2,6]{4,3,2,1,0,9,8,7,6,5:T(2,128)} %reshape.514) | data formatting | bytes 165888 | tf_op jit(solution)/shard_map/reshape | solution.py:43
  21.7 0.0 copy-start.13
  21.7 2.6 %reshape.515 = s32[144,144]{1,0:T(8,128)} reshape(s32[2,2,2,3,6,2,2,2,3,6]{9,8,7,6,5,4,3,2,1,0:T(4,128)S(1)} %bitcast.40) | data formatting | bytes 165888 | tf_op jit(solution)/shard_map/reshape | solution.py:45
  24.3 0.1 compare_select_fusion.4
  24.4 0.1 select_reduce_fusion
  24.5 0.0 slice-start
  24.5 1.1 %copy.38 = bf16[2,2,12,3312]{3,2,1,0:T(8,128)(2,1)S(1)} copy(bf16[2,2,12,3312]{3,1,2,0:T(2,128)(2,1)} %param.22) | data formatting | bytes 635904 | tf_op args[9]
  25.6 0.1 reshape.511
  25.8 0.2 reshape.512
  26.0 0.1 copy.39
  26.1 0.1 concatenate.62
  26.2 0.4 and_select_fusion
  26.6 0.1 and_select_fusion.1.low_ref
  26.7 0.0 copy-start.10
  26.8 0.0 copy-start.11
  26.8 0.0 copy-start.12
  26.8 0.0 copy-start.3
  26.8 10.3 %bias_lookup.1 = (f32[6912,128]{1,0:T(8,128)S(1)}, f32[6912,128]{1,0:T(8,128)S(1)}) custom-call(bf16[624,256]{1,0:T(8,128)(2,1)S(1)} %bitcast.32, s32[81,1,256]{2,1,0:T(1,128)S(1)} %and_select_fusion.1.low_ref, s32[81,1,256]{2,1,0:T(1,128)S(1)} %get-tuple-element.29.high_ref), custom_call_target="tpu_custom_call" | custom-call | flops 6624903168 | bytes 8388608 | tf_op jit(solution)/shard_map/bias_lookup/pallas_call | solution.py:144
  37.1 1.7 %copy-done.7 = f32[6912,128]{1,0:T(8,128)} copy-done((f32[6912,128]{1,0:T(8,128)}, f32[6912,128]{1,0:T(8,128)S(1)}, u32[]{:S(2)}) %copy-start.7) | copy-done | bytes 3538968
  38.9 1.8 %copy-done.8 = f32[6912,128]{1,0:T(8,128)} copy-done((f32[6912,128]{1,0:T(8,128)}, f32[6912,128]{1,0:T(8,128)S(1)}, u32[]{:S(2)}) %copy-start.8) | copy-done | bytes 3538968
  40.7 0.9 %slice_bitcast_fusion.1 = bf16[2,36,768]{2,1,0:T(8,128)(2,1)S(1)} fusion(bf16[2,2,36,768]{3,2,0,1:T(8,128)(2,1)} %collective-permute-done), kind=kLoop, calls=%fused_computation.7 | loop fusion | bytes 221184 | tf_op jit(solution)/shard_map/squeeze | solution.py:355
  41.6 0.8 collective-permute-start.2
  42.4 0.1 copy.45.key_ref
  42.6 0.1 copy.43.key_ref
  42.7 1.0 %copy.42.own_last_ref = bf16[2,2,36,768]{3,2,1,0:T(8,128)(2,1)S(1)} copy(bf16[2,2,36,768]{3,2,0,1:T(8,128)(2,1)} %collective-permute-done) | data formatting | bytes 442368 | tf_op jit(solution)/shard_map/ppermute | solution.py:27
  43.7 0.0 collective-permute-done.1.halo_ref
  43.7 3.6 %collective-permute-done.2.halo_last_ref = bf16[2,36,768]{2,1,0:T(8,128)(2,1)S(1)} collective-permute-done((bf16[2,36,768]{2,1,0:T(8,128)(2,1)S(1)}, bf16[2,36,768]{2,1,0:T(8,128)(2,1)S(1)}, u32[]{:S(2)}, u32[]{:S(2)}) %collective-permute-start.2) | collective-permute-done | bytes 110624 | tf_op jit(solution)/shard_map/ppermute | solution.py:27
  47.3 1.1 %copy-done.4 = bf16[384,768]{1,0:T(8,128)(2,1)S(1)} copy-done((bf16[384,768]{1,0:T(8,128)(2,1)S(1)}, bf16[384,768]{1,0:T(8,128)(2,1)}, u32[]{:S(2)}) %copy-start.4) | copy-done | bytes 589848
  48.4 1.0 %copy-done.6 = bf16[2,108,768]{2,1,0:T(8,128)(2,1)S(1)} copy-done((bf16[2,108,768]{2,1,0:T(8,128)(2,1)S(1)}, bf16[2,108,768]{2,1,0:T(8,128)(2,1)}, u32[]{:S(2)}) %copy-start.6) | copy-done | bytes 331800
  49.3 8.7 %window_attention.3 = (bf16[108,768]{1,0:T(8,128)(2,1)S(1)}, bf16[108,768]{1,0:T(8,128)(2,1)S(1)}, bf16[2,36,768]{2,1,0:T(8,128)(2,1)S(1)}) custom-call(bf16[2,108,768]{2,1,0:T(8,128)(2,1)S(1)} %copy-done.6, bf16[2,2,36,768]{3,2,1,0:T(8,128)(2,1)S(1)} %copy.42.own_last_ref, bf16[2,108,768]{2,1,0:T(8,128)(2,1)} %collective-permute-done.1.halo_ref, ...), custom_call_target="tpu_custom_call" | custom-call | flops 6000000000 | bytes 8388608 | tf_op jit(solution)/shard_map/window_attention/pallas_call | solution.py:244
  58.0 0.0 copy-start
  58.0 8.7 %window_attention.2 = (bf16[108,768]{1,0:T(8,128)(2,1)S(1)}, bf16[108,768]{1,0:T(8,128)(2,1)S(1)}, bf16[2,36,768]{2,1,0:T(8,128)(2,1)S(1)}) custom-call(bf16[2,108,768]{2,1,0:T(8,128)(2,1)S(1)} %copy-done.6, bf16[2,2,36,768]{3,2,1,0:T(8,128)(2,1)S(1)} %copy.42.own_last_ref, bf16[2,108,768]{2,1,0:T(8,128)(2,1)} %collective-permute-done.1.halo_ref, ...), custom_call_target="tpu_custom_call" | custom-call | flops 6000000000 | bytes 8388608 | tf_op jit(solution)/shard_map/window_attention/pallas_call | solution.py:244
  66.8 0.1 collective-permute-start.4
  66.8 0.1 collective-permute-start.6
  66.9 0.1 collective-permute-start.3
  67.0 1.4 %collective-permute-done.4 = bf16[2,2,36,768]{3,2,1,0:T(8,128)(2,1)S(1)} collective-permute-done((bf16[2,2,36,768]{3,2,1,0:T(8,128)(2,1)S(1)}, bf16[2,2,36,768]{3,2,1,0:T(8,128)(2,1)S(1)}, u32[]{:S(2)}, u32[]{:S(2)}) %collective-permute-start.4) | collective-permute-done | bytes 221216 | tf_op jit(solution)/shard_map/ppermute | solution.py:27
  68.4 0.1 collective-permute-start.5
  68.4 14.2 %collective-permute-done.5 = bf16[2,36,768]{2,1,0:T(8,128)(2,1)S(1)} collective-permute-done((bf16[2,36,768]{2,1,0:T(8,128)(2,1)S(1)}, bf16[2,36,768]{2,1,0:T(8,128)(2,1)S(1)}, u32[]{:S(2)}, u32[]{:S(2)}) %collective-permute-start.5) | collective-permute-done | bytes 110624 | tf_op jit(solution)/shard_map/ppermute | solution.py:27
  82.7 0.8 unpack_and_add.1
  83.5 1.6 %copy.46 = bf16[4,12,12,768]{3,0,2,1:T(4,128)(2,1)} copy(bf16[4,12,12,768]{3,2,1,0:T(8,128)(2,1)S(1)} %unpack_and_add.1) | data formatting | bytes 1769472 | tf_op jit(solution)/shard_map/unpack_and_add/pallas_call | solution.py:326
  (39 shorter events, 0.2 us)
Async XLA Ops:
  0.0 2.2 %copy-start.1 = (bf16[320,384]{1,0:T(8,128)(2,1)S(1)}, bf16[320,384]{1,0:T(8,128)(2,1)}, u32[]{:S(2)}) copy-start(bf16[320,384]{1,0:T(8,128)(2,1)} %constant.111.clone.chosen_ref) | copy-start | bytes 737284
  0.0 2.2 %copy-start.2 = (f32[2,768]{1,0:T(2,128)S(1)}, f32[2,768]{1,0:T(2,128)}, u32[]{:S(2)}) copy-start(f32[2,768]{1,0:T(2,128)} %embed_ref.1) | copy-start | bytes 18436
  0.8 9.9 %copy-start.9 = (s32[144,144]{1,0:T(8,128)S(1)}, s32[144,144]{1,0:T(8,128)}, u32[]{:S(2)}) copy-start(s32[144,144]{1,0:T(8,128)} %param.23) | copy-start | bytes 248836
  3.8 0.9 %copy-start.5 = (bf16[2,108,768]{2,1,0:T(8,128)(2,1)}, bf16[2,108,768]{2,1,0:T(8,128)(2,1)S(1)}, u32[]{:S(2)}) copy-start(bf16[2,108,768]{2,1,0:T(8,128)(2,1)S(1)} %get-tuple-element.18.own_ref) | copy-start | bytes 995332
  4.7 36.0 %collective-permute-start = (bf16[2,2,36,768]{3,2,0,1:T(8,128)(2,1)}, bf16[2,2,36,768]{3,2,0,1:T(8,128)(2,1)}, u32[]{:S(2)}, u32[]{:S(2)}) collective-permute-start(bf16[2,2,36,768]{3,2,0,1:T(8,128)(2,1)} %copy.37), channel_id=1, source_target_pairs={{0,1},{1,0},{2,3},{3,2},{4,5},{5,4},{6,7},{7,6},{8,9},{9,8},{10,11... | collective-permute-start | bytes 663560 | tf_op jit(solution)/shard_map/ppermute | solution.py:27
  5.2 38.5 %collective-permute-start.1 = (bf16[2,108,768]{2,1,0:T(8,128)(2,1)}, bf16[2,108,768]{2,1,0:T(8,128)(2,1)}, u32[]{:S(2)}, u32[]{:S(2)}) collective-permute-start(bf16[2,108,768]{2,1,0:T(8,128)(2,1)} %get-tuple-element.20), channel_id=1, source_target_pairs={{0,14},{2,0},{4,2},{6,4},{8,6},{10,8},{12,10},{14,12},{1,15},{3,1}... | collective-permute-start | bytes 995336 | tf_op jit(solution)/shard_map/ppermute | solution.py:27
  21.7 2.7 %copy-start.13 = (s32[24]{0:T(128)S(1)}, s32[24]{0:T(128)}, u32[]{:S(2)}) copy-start(s32[24]{0:T(128)} %param.15) | copy-start | bytes 292
  24.5 1.6 %slice-start = ((s32[144,144]{1,0:T(8,128)}), s32[144,16]{1,0:T(8,128)S(1)}, s32[]{:S(2)}) async-start(s32[144,144]{1,0:T(8,128)} %reshape.515), calls=%async_computation | async-start | bytes 147456 | tf_op jit(solution)/shard_map/slice | solution.py:141
  24.5 1.7 %slice-start.1 = ((s32[144,144]{1,0:T(8,128)}), s32[144,128]{1,0:T(8,128)S(1)}, s32[]{:S(2)}) async-start(s32[144,144]{1,0:T(8,128)} %reshape.515), calls=%async_computation.1 | async-start | bytes 147456 | tf_op jit(solution)/shard_map/slice | solution.py:140
  26.7 15.6 %copy-start.10 = (f32[768]{0:T(1024)S(1)}, f32[768]{0:T(1024)}, u32[]{:S(2)}) copy-start(f32[768]{0:T(1024)} %param.19) | copy-start | bytes 9220
  26.8 15.6 %copy-start.11 = (f32[768]{0:T(1024)S(1)}, f32[768]{0:T(1024)}, u32[]{:S(2)}) copy-start(f32[768]{0:T(1024)} %param.20) | copy-start | bytes 9220
  26.8 15.6 %copy-start.12 = (f32[768]{0:T(1024)S(1)}, f32[768]{0:T(1024)}, u32[]{:S(2)}) copy-start(f32[768]{0:T(1024)} %param.21) | copy-start | bytes 9220
  26.8 20.5 %copy-start.3 = (bf16[768,1152]{1,0:T(8,128)(2,1)S(1)}, bf16[768,1152]{1,0:T(8,128)(2,1)}, u32[]{:S(2)}) copy-start(bf16[768,1152]{1,0:T(8,128)(2,1)} %w_qkv_ref.3) | copy-start | bytes 5308420
  37.1 1.7 %copy-start.7 = (f32[6912,128]{1,0:T(8,128)}, f32[6912,128]{1,0:T(8,128)S(1)}, u32[]{:S(2)}) copy-start(f32[6912,128]{1,0:T(8,128)S(1)} %get-tuple-element.21) | copy-start | bytes 10616836
  38.9 1.8 %copy-start.8 = (f32[6912,128]{1,0:T(8,128)}, f32[6912,128]{1,0:T(8,128)S(1)}, u32[]{:S(2)}) copy-start(f32[6912,128]{1,0:T(8,128)S(1)} %get-tuple-element.22) | copy-start | bytes 10616836
  41.6 5.7 %collective-permute-start.2 = (bf16[2,36,768]{2,1,0:T(8,128)(2,1)S(1)}, bf16[2,36,768]{2,1,0:T(8,128)(2,1)S(1)}, u32[]{:S(2)}, u32[]{:S(2)}) collective-permute-start(bf16[2,36,768]{2,1,0:T(8,128)(2,1)S(1)} %slice_bitcast_fusion.1), channel_id=1, source_target_pairs={{0,14},{2,0},{4,2},{6,4},{8,6},{10,8},{12,10},{14,12},{1,15},{3,1}... | collective-permute-start | bytes 331784 | tf_op jit(solution)/shard_map/ppermute | solution.py:27
  47.3 1.1 %copy-start.4 = (bf16[384,768]{1,0:T(8,128)(2,1)S(1)}, bf16[384,768]{1,0:T(8,128)(2,1)}, u32[]{:S(2)}) copy-start(bf16[384,768]{1,0:T(8,128)(2,1)} %w_proj_ref.3) | copy-start | bytes 1769476
  48.3 1.0 %copy-start.6 = (bf16[2,108,768]{2,1,0:T(8,128)(2,1)S(1)}, bf16[2,108,768]{2,1,0:T(8,128)(2,1)}, u32[]{:S(2)}) copy-start(bf16[2,108,768]{2,1,0:T(8,128)(2,1)} %copy-done.5) | copy-start | bytes 995332
  58.0 24.7 %copy-start = (bf16[384,320]{1,0:T(8,128)(2,1)S(1)}, bf16[384,320]{1,0:T(8,128)(2,1)}, u32[]{:S(2)}) copy-start(bf16[384,320]{1,0:T(8,128)(2,1)} %constant.112.clone.chosen_ref) | copy-start | bytes 737284
  66.8 1.6 %collective-permute-start.4 = (bf16[2,2,36,768]{3,2,1,0:T(8,128)(2,1)S(1)}, bf16[2,2,36,768]{3,2,1,0:T(8,128)(2,1)S(1)}, u32[]{:S(2)}, u32[]{:S(2)}) collective-permute-start(bf16[2,2,36,768]{3,2,1,0:T(8,128)(2,1)S(1)} %pad_maximum_fusion), channel_id=1, source_target_pairs={{0,1},{1,0},{2,3},{3,2},{4,5},{5,4},{6,7},{7,6},{8,9},{9,8},{10,11... | collective-permute-start | bytes 663560 | tf_op jit(solution)/shard_map/ppermute | solution.py:27
  66.8 15.8 %collective-permute-start.6 = (bf16[108,768]{1,0:T(8,128)(2,1)S(1)}, bf16[108,768]{1,0:T(8,128)(2,1)S(1)}, u32[]{:S(2)}, u32[]{:S(2)}) collective-permute-start(bf16[108,768]{1,0:T(8,128)(2,1)S(1)} %get-tuple-element.27), channel_id=1, source_target_pairs={{0,2},{2,4},{4,6},{6,8},{8,10},{10,12},{12,14},{14,0},{1,3},{3,5},... | collective-permute-start | bytes 497672 | tf_op jit(solution)/shard_map/ppermute | solution.py:27
  66.9 15.8 %collective-permute-start.3 = (bf16[108,768]{1,0:T(8,128)(2,1)S(1)}, bf16[108,768]{1,0:T(8,128)(2,1)S(1)}, u32[]{:S(2)}, u32[]{:S(2)}) collective-permute-start(bf16[108,768]{1,0:T(8,128)(2,1)S(1)} %get-tuple-element.23), channel_id=1, source_target_pairs={{0,2},{2,4},{4,6},{6,8},{8,10},{10,12},{12,14},{14,0},{1,3},{3,5},... | collective-permute-start | bytes 497672 | tf_op jit(solution)/shard_map/ppermute | solution.py:27
  68.4 14.3 %collective-permute-start.5 = (bf16[2,36,768]{2,1,0:T(8,128)(2,1)S(1)}, bf16[2,36,768]{2,1,0:T(8,128)(2,1)S(1)}, u32[]{:S(2)}, u32[]{:S(2)}) collective-permute-start(bf16[2,36,768]{2,1,0:T(8,128)(2,1)S(1)} %slice_bitcast_fusion), channel_id=1, source_target_pairs={{0,2},{2,4},{4,6},{6,8},{8,10},{10,12},{12,14},{14,0},{1,3},{3,5},... | collective-permute-start | bytes 331784 | tf_op jit(solution)/shard_map/ppermute | solution.py:27
